TPU v7x, 256 devices: a whole 4x4x8 slice. The times are simulated.
256 devices in a mesh: row: 64 (over x, z, core), col: 4 (over y).
Axes of the slice: x: 4, y: 4, z: 8, core: 2. Of those that a mesh axis runs over, the one named last changes fastest.
Arguments:
- a_values: bfloat16 [16384, 16384], P('row', 'col'), may hold values from -0.046875 to 0.046875
- a_present: int32 [64, 64], P('row', 'col'), may hold values from 0 to 1, as said below
- b_values: bfloat16 [16384, 2048], P('row', 'col'), may hold values from -6 to 6
- b_present: int32 [64, 8], P('row', 'col'), may hold values 0 or 1
- w_values: bfloat16 [16384, 2048], P('row', 'col'), may hold values from -6 to 6
- w_present: int32 [64, 8], P('row', 'col'), may hold values 0 or 1
Outputs:
- masked: bfloat16 [16384, 2048], P('row', 'col')
- slot: float32 [64, 8], P('row', 'col')
- total: float32 [], replicated
Inputs may be any that keep to these rules, and one draw needn't show every extreme that they name: `a_present`: 1 where a tile of a_values is present, else 0; the share of present tiles differs strongly from tile row to tile row.
All inputs are finite; a program needn't handle non-finite values. No bound on the sum of `b_present` or of `w_present` on one device may be relied on, other than what follows from the above.
Results may differ from a plain program's by a relative error of at most 0.001.
Values may be sent and summed in bfloat16 or wider, within the bound.
A program may use at most 128 MiB of HBM per device.

v0:
```python
import functools
import math

import jax
import jax.numpy as jnp
from jax import lax
from jax.sharding import Mesh
from jax.sharding import PartitionSpec as P

TILE = 256
ROW = ("row_0", "row_1", "row_2")
ROW_COL = ("row_0", "row_1", "row_2", "col")


def sent_to_all(array, axis):
    copies = jnp.broadcast_to(array, (lax.axis_size(axis), *array.shape))
    return lax.all_to_all(copies, axis, split_axis=0, concat_axis=0, tiled=True)


def laid_out(blocks, dim):
    blocks = jnp.moveaxis(blocks, 0, dim)
    dims = blocks.shape
    return blocks.reshape(*dims[:dim], dims[dim] * dims[dim + 1], *dims[dim + 2 :])


def gathered_copies(array, axis, dim):
    blocks = sent_to_all(array, axis)
    return laid_out(blocks, dim)


def nothing_yet(array, identity):
    return jnp.broadcast_to(jnp.asarray(identity, array.dtype), array.shape)


def entering(array, axes, combine, identity):
    before = start = nothing_yet(array, identity)
    subtotal = array
    for axis in reversed(axes):
        peers, place = (lax.axis_size(axis), lax.axis_index(axis))
        pieces = lax.all_gather(subtotal, axis)
        inside, subtotal = (start, start)
        for k in range(peers):
            passed = k < place
            subtotal = combine(subtotal, pieces[k])
            inside = jnp.where(passed, subtotal, inside)
        before = combine(inside, before)
    return before


def by_axis(array, axes):
    return functools.reduce(lax.psum, axes, array)


def expand(values, present):
    tile_rows, tile_cols = present.shape
    tile_size = values.shape[0] // tile_rows
    blocked = values.reshape(tile_rows, tile_size, tile_cols, tile_size)
    masked_tiles = blocked * present.astype(values.dtype)[:, None, :, None]
    return masked_tiles.reshape(values.shape)


def add_counts(earlier, later):
    return earlier + later


def on_device(a_values, a_present, b_values, b_present, w_values, w_present):
    tile_size = TILE
    row_tiles, inner_local = a_present.shape
    b_row_tiles, col_tiles = b_present.shape
    a_eff = expand(a_values, a_present)
    b_eff = expand(b_values, b_present).reshape(b_row_tiles, tile_size, col_tiles * tile_size)
    w_eff = expand(w_values, w_present).astype(jnp.float32)
    a_full, a_mask = (gathered_copies(a_eff, "col", 1), gathered_copies(a_present, "col", 1))
    b_piece = lax.all_gather(b_eff, ROW, axis=0, tiled=True)
    b_mask = lax.all_gather(b_present, ROW, axis=0, tiled=True)
    count_tiles = b_mask.shape[0]
    new_prod = jnp.dot(
        a_full,
        b_piece.reshape(count_tiles * tile_size, col_tiles * tile_size),
        preferred_element_type=jnp.float32,
    )
    new_link = jnp.dot(a_mask, b_mask, preferred_element_type=jnp.int32)
    weighted = new_prod * w_eff
    masked = weighted.astype(jnp.bfloat16)
    local_sum = jnp.sum(weighted)
    present = w_present * (new_link > 0).astype(jnp.int32)
    flat_present = present.reshape(-1)
    tile_count = jnp.sum(flat_present)
    tile_rank = jnp.cumsum(flat_present) - flat_present
    first_slot = entering(tile_count, ROW_COL, add_counts, jnp.int32(0))
    whole_sum = by_axis(local_sum, ROW_COL)
    slot = (
        jnp.where(flat_present > 0, first_slot + tile_rank, -1)
        .astype(jnp.int32)
        .reshape(row_tiles, col_tiles)
    )
    norm_scale = tile_size * math.sqrt(
        row_tiles * lax.axis_size(ROW) * col_tiles * lax.axis_size("col")
    )
    total = whole_sum / norm_scale
    return (masked, slot.astype(jnp.float32), total)


def solution(mesh):
    split = Mesh(
        mesh.devices.reshape(4, 8, 2, mesh.shape["col"]), ("row_0", "row_1", "row_2", "col")
    )
    return jax.shard_map(
        on_device,
        mesh=split,
        in_specs=(
            P(ROW, "col"),
            P(ROW, "col"),
            P(ROW, "col"),
            P(ROW, "col"),
            P(ROW, "col"),
            P(ROW, "col"),
        ),
        out_specs=(P(ROW, "col"), P(ROW, "col"), P()),
        check_vma=False,
    )
```

profile of v0, /device:TPU:1, one launch (start us, length us, event | category | flops | bytes accessed | tf_op | source)
XLA Modules:
  0.0 233.3 jit_solution(11051457864793521886)
XLA Ops:
  8.0 1.7 broadcast_multiply_fusion.1
  9.6 1.2 broadcast_in_dim.14
  10.9 5.0 %all-to-all-start.1 = ((s32[4,1,16]{2,1,0:T(1,128)}), s32[4,1,16]{2,1,0:T(1,128)S(1)}, u32[]{:S(2)}, u32[]{:S(2)}) async-start(s32[4,1,16]{2,1,0:T(1,128)} %broadcast_in_dim.14), calls=%async_computation.1 | async-start | bytes 4096 | tf_op jit(solution)/shard_map/all_to_all | solution.py:17
  16.6 3.1 %broadcast_multiply_fusion = bf16[256,4096]{1,0:T(8,128)(2,1)} fusion(bf16[256,4096]{1,0:T(8,128)(2,1)} %param.6, bf16[4096]{0:T(1024)(128)(2,1)S(1)} %bitcast.65), kind=kLoop, calls=%fused_computation.5 | loop fusion | flops 1048576 | bytes 4202496 | tf_op jit(solution)/shard_map/mul | solution.py:58
  19.7 3.3 %copy.12 = bf16[256,4096]{0,1:T(8,128)(2,1)S(1)} copy(bf16[256,4096]{1,0:T(8,128)(2,1)} %broadcast_multiply_fusion) | data formatting | bytes 4194304 | tf_op jit(solution)/shard_map/mul | solution.py:58
  23.0 3.7 %broadcast_in_dim.13 = bf16[4,256,4096]{1,2,0:T(8,128)(2,1)} broadcast(bf16[256,4096]{0,1:T(8,128)(2,1)S(1)} %copy.12), dimensions={1,2} | broadcast | bytes 10485760 | tf_op jit(solution)/shard_map/broadcast_in_dim | solution.py:16
  26.8 5.8 %all-to-all-start = ((bf16[4,256,4096]{1,2,0:T(8,128)(2,1)}), bf16[4,256,4096]{1,2,0:T(8,128)(2,1)}, u32[]{:S(2)}, u32[]{:S(2)}) async-start(bf16[4,256,4096]{1,2,0:T(8,128)(2,1)} %broadcast_in_dim.13), calls=%async_computation | async-start | bytes 16777216 | tf_op jit(solution)/shard_map/all_to_all | solution.py:17
  35.2 43.8 %all-gather.1 = s32[64,1,2]{2,1,0:T(1,128)S(1)} all-gather(s32[1,1,2]{2,1,0:T(1,128)S(1)} %bitcast.68), channel_id=1, replica_groups=mesh['row_0'=4,'row_1'=8,'row_2'=2,'col'=4] {'row_0','row_1','row_2'}, dimensions={0}, use_global_device_ids=true | all-gather | bytes 520 | tf_op jit(solution)/shard_map/all_gather | solution.py:75
  79.6 0.7 reduce.4
  80.3 0.8 fusion.9
  81.1 1.4 dynamic-update-slice
  82.6 44.5 %all-reduce = s32[4]{0:T(128)S(1)} all-reduce(s32[4]{0:T(128)S(1)} %dynamic-update-slice), channel_id=1, replica_groups=mesh['row_0'=4,'row_1'=8,'row_2'=2,'col'=4] {'col'}, use_global_device_ids=true, to_apply=%add | all-reduce | flops 4 | bytes 32
  130.2 0.7 dynamic-update-slice.1
  130.9 4.5 %all-reduce.1 = s32[2]{0:T(128)S(1)} all-reduce(s32[2]{0:T(128)S(1)} %dynamic-update-slice.1), channel_id=1, replica_groups=mesh['row_0'=4,'row_1'=8,'row_2'=2,'col'=4] {'row_2'}, use_global_device_ids=true, to_apply=%add.1 | all-reduce | flops 2 | bytes 16
  137.3 0.7 dynamic-update-slice.2
  138.0 13.2 %all-reduce.2 = s32[8]{0:T(128)S(1)} all-reduce(s32[8]{0:T(128)S(1)} %dynamic-update-slice.2), channel_id=1, replica_groups=mesh['row_0'=4,'row_1'=8,'row_2'=2,'col'=4] {'row_1'}, use_global_device_ids=true, to_apply=%add.2 | all-reduce | flops 8 | bytes 64
  156.6 0.8 dynamic-update-slice.3
  157.4 6.9 %all-reduce.3 = s32[4]{0:T(128)S(1)} all-reduce(s32[4]{0:T(128)S(1)} %dynamic-update-slice.3), channel_id=1, replica_groups=mesh['row_0'=4,'row_1'=8,'row_2'=2,'col'=4] {'row_0'}, use_global_device_ids=true, to_apply=%add.3 | all-reduce | flops 4 | bytes 32
  164.5 0.7 fusion.5
  170.2 14.0 %fusion.4 = (f32[]{:T(128)}, bf16[256,512]{1,0:T(8,128)(2,1)}) fusion(bf16[256,512]{1,0:T(8,128)(2,1)S(1)} %copy-done, bf16[512]{0:T(512)(128)(2,1)S(1)} %bitcast.66, bf16[256,16384]{0,1:T(8,128)(2,1)} %bitcast.2, bf16[16384,512]{1,0:T(8,128)(2,1)} %all-gather.4.cloned.1.call-done), kind=kOutput, calls=%fused_computation.15 | convolution fusion | flops 4295622656 | bytes 25691140 | tf_op jit(solution)/shard_map/dot_general | solution.py:77
  184.2 7.5 %psum.28 = f32[]{:T(128)} all-reduce(f32[]{:T(128)} %get-tuple-element.3), channel_id=1, replica_groups=mesh['row_0'=4,'row_1'=8,'row_2'=2,'col'=4] {'row_0'}, use_global_device_ids=true, to_apply=%region_3.4 | all-reduce | flops 1 | bytes 8 | tf_op jit(solution)/shard_map/psum | solution.py:51
  191.7 12.0 %psum.29 = f32[]{:T(128)} all-reduce(f32[]{:T(128)} %psum.28), channel_id=1, replica_groups=mesh['row_0'=4,'row_1'=8,'row_2'=2,'col'=4] {'row_1'}, use_global_device_ids=true, to_apply=%region_4.5 | all-reduce | flops 1 | bytes 8 | tf_op jit(solution)/shard_map/psum | solution.py:51
  203.7 13.8 %psum.30 = f32[]{:T(128)} all-reduce(f32[]{:T(128)} %psum.29), channel_id=1, replica_groups=mesh['row_0'=4,'row_1'=8,'row_2'=2,'col'=4] {'row_2'}, use_global_device_ids=true, to_apply=%region_5.6 | all-reduce | flops 1 | bytes 8 | tf_op jit(solution)/shard_map/psum | solution.py:51
  218.0 6.7 %psum.31 = f32[]{:T(128)} all-reduce(f32[]{:T(128)} %psum.30), channel_id=1, replica_groups=mesh['row_0'=4,'row_1'=8,'row_2'=2,'col'=4] {'col'}, use_global_device_ids=true, to_apply=%region_6.7 | all-reduce | flops 1 | bytes 8 | tf_op jit(solution)/shard_map/psum | solution.py:51
  (43 shorter events, 7.3 us)
Async XLA Ops:
  7.2 163.0 %all-gather.4.cloned.1.call-start = ((), (), s32[]{:S(2)}) async-start(), calls=%async_computation.2 | async-start | bytes 17039360 | tf_op jit(solution)/shard_map/all_gather | solution.py:74
  10.9 12.1 %all-to-all-start.1 = ((s32[4,1,16]{2,1,0:T(1,128)}), s32[4,1,16]{2,1,0:T(1,128)S(1)}, u32[]{:S(2)}, u32[]{:S(2)}) async-start(s32[4,1,16]{2,1,0:T(1,128)} %broadcast_in_dim.14), calls=%async_computation.1 | async-start | bytes 4096 | tf_op jit(solution)/shard_map/all_to_all | solution.py:17
  26.7 5.9 %copy-start.2 = (s32[1,2]{1,0:T(1,128)S(1)}, s32[1,2]{1,0:T(1,128)}, u32[]{:S(2)}) copy-start(s32[1,2]{1,0:T(1,128)} %param.11) | copy-start | bytes 28
  26.8 6.0 %copy-start.6 = (u32[256]{0:T(256)S(1)}, u32[256]{0:T(256)}, u32[]{:S(2)}) copy-start(u32[256]{0:T(256)} %constant.51) | copy-start | bytes 3076
  26.8 6.6 %copy-start.5 = (u32[256]{0:T(256)S(1)}, u32[256]{0:T(256)}, u32[]{:S(2)}) copy-start(u32[256]{0:T(256)} %constant.56) | copy-start | bytes 3076
  26.8 7.2 %copy-start.4 = (u32[256]{0:T(256)S(1)}, u32[256]{0:T(256)}, u32[]{:S(2)}) copy-start(u32[256]{0:T(256)} %constant.61) | copy-start | bytes 3076
  26.8 7.8 %copy-start.3 = (u32[256]{0:T(256)S(1)}, u32[256]{0:T(256)}, u32[]{:S(2)}) copy-start(u32[256]{0:T(256)} %constant.66) | copy-start | bytes 3076
  26.8 8.5 %copy-start.1 = (s32[1,2]{1,0:T(1,128)S(1)}, s32[1,2]{1,0:T(1,128)}, u32[]{:S(2)}) copy-start(s32[1,2]{1,0:T(1,128)} %param.9) | copy-start | bytes 28
  26.8 143.4 %copy-start = (bf16[256,512]{1,0:T(8,128)(2,1)S(1)}, bf16[256,512]{1,0:T(8,128)(2,1)}, u32[]{:S(2)}) copy-start(bf16[256,512]{1,0:T(8,128)(2,1)} %param.10) | copy-start | bytes 786436
  26.8 143.4 %all-to-all-start = ((bf16[4,256,4096]{1,2,0:T(8,128)(2,1)}), bf16[4,256,4096]{1,2,0:T(8,128)(2,1)}, u32[]{:S(2)}, u32[]{:S(2)}) async-start(bf16[4,256,4096]{1,2,0:T(8,128)(2,1)} %broadcast_in_dim.13), calls=%async_computation | async-start | bytes 16777216 | tf_op jit(solution)/shard_map/all_to_all | solution.py:17
Sparse Core Ops, SparseCore 0:
  11.3 103.3 all-gather.3
where the time goes:
time: 235 us; the launch traced here: 233 us
  blocking collectives  153 us (65%)
  between operations  29.5 us (13%)
  local copies, waits for them, and re-layouts  17.8 us (8%)
  matrix products  14.8 us (6%)
  starting transfers between devices  10.8 us (5%)
  other arithmetic  7.43 us (3%)
    unnamed x4, blocking collectives  69.2 us
    all_gather x1, blocking collectives, on_device(): b_mask = lax.all_gather(b_present, ROW, axis=0, tiled=True)  43.8 us
    psum x4, blocking collectives, by_axis(): return functools.reduce(lax.psum, axes, array)  39.9 us
    dot_general x1, matrix products, on_device(): jnp.dot(a_full, b_piece.reshape(count_tiles * tile_size, col_tiles * tile...  14 us
    all_to_all x2, starting transfers between devices, sent_to_all(): return lax.all_to_all(copies, axis, split_axis=0, concat_axis=0, tiled=True)  10.8 us
    unnamed x31, local copies, waits for them, and re-layouts  6.43 us
    mul x5, other arithmetic, expand(): masked_tiles = blocked * present.astype(values.dtype)[:, None, :, None]  6.08 us
    broadcast_in_dim x2, local copies, waits for them, and re-layouts, sent_to_all(): copies = jnp.broadcast_to(array, (lax.axis_size(axis), *array.shape))  4.98 us
  transfers between devices with their start and end apart: 3, of which 0 were waited for; matrix products, arithmetic and copies ran while one was open for 10% of the time, Pallas kernels for 0%

commit v1 on v0

v1 whole, which is shorter than its diff:
```python
import functools
import heapq
import math

import jax
import jax.numpy as jnp
from jax import lax
from jax.experimental import pallas as pl
from jax.experimental.pallas import tpu as pltpu
from jax.sharding import PartitionSpec as P

MESH = pl.DeviceIdType.MESH
TILE = 256
NX, NZ, NY = 4, 8, 4
BLOCK = 1024
N1 = 384
ROWS = ((0, N1), (N1, BLOCK))
LINKS = ("x+", "x-", "z+", "z-")
LATENCY, RATE, LEAD = 2.2, 46.6e3, 3.0
RELAY = (0, -1, 2, -3)


def span(key):
    half, _, _, part = key
    first, last = ROWS[half]
    middle = (first + last) // 2
    return {"f": (first, last), "a": (first, middle), "b": (middle, last)}[part]


def plan():
    free = dict.fromkeys(LINKS, 0.0)
    waiting = {link: [] for link in LINKS}
    events, arrived, steps, count = [], {}, [], [0]

    def want(link, key, rank):
        count[0] += 1
        heapq.heappush(waiting[link], (rank, count[0], key))

    def send(now):
        out = []
        for link in LINKS:
            while waiting[link] and free[link] - now < LEAD:
                _, _, key = heapq.heappop(waiting[link])
                first, last = span(key)
                free[link] = max(now, free[link]) + (last - first) * 256 / RATE
                count[0] += 1
                heapq.heappush(events, (free[link] + LATENCY, count[0], key))
                out.append((link, key))
        return out

    def along_z(half, dx, dz):
        rank = abs(dx) if half == 0 else -1
        if dz == 0:
            want("z+", (half, dx, -1, "f"), rank)
            want("z-", (half, dx, 1, "f"), rank)
            return
        sign, link = (-1, "z+") if dz < 0 else (1, "z-")
        if abs(dz) < 3:
            want(link, (half, dx, dz + sign, "f"), rank)
        else:
            want(link, (half, dx, 4, "a" if sign < 0 else "b"), rank)

    along_z(1, 0, 0)
    want("x+", (0, -1, 0, "f"), -1)
    want("x-", (0, 1, 0, "f"), -1)
    along_z(0, 0, 0)
    want("x+", (1, -1, 0, "f"), 1)
    want("x-", (1, 1, 0, "f"), 1)
    steps.append((0.0, None, send(0.0)))
    while events:
        now, _, key = heapq.heappop(events)
        arrived[key] = now
        half, dx, dz, part = key
        whole = part == "f" or all((half, dx, dz, p) in arrived for p in "ab")
        if half == 0:
            if dz == 0:
                if dx == -1:
                    want("x+", (0, 2, 0, "a"), 0)
                if dx == 1:
                    want("x-", (0, 2, 0, "b"), 0)
                if whole:
                    along_z(0, dx, 0)
            elif part == "f":
                along_z(0, dx, dz)
        elif dx == 0:
            if part == "f":
                along_z(1, 0, dz)
            if whole:
                want("x+", (1, -1, dz, "f"), 1)
                want("x-", (1, 1, dz, "f"), 1)
        elif dx == -1 and dz in RELAY:
            want("x+", (1, 2, dz, "f"), 2)
        elif dx == 1 and dz not in RELAY:
            want("x-", (1, 2, dz, "f"), 2)
        steps.append((now, key, send(now)))
    return steps, arrived


STEPS, ARRIVED = plan()
KEYS = {key: n for n, key in enumerate(sorted(ARRIVED))}
BLOCKS = [(dx, dz) for dx in (0, -1, 1, 2) for dz in (0, -1, 1, -2, 2, -3, 3, 4)]
BLOCK_ID = {block: n for n, block in enumerate(BLOCKS)}
GROUP = {0: 0, -1: 1, 1: 2, 2: 3}


def program():
    items, need = [], {block: 0 for block in BLOCKS}
    for key in ARRIVED:
        need[key[1], key[2]] += 1
    complete = {}
    for now, key, sends in STEPS:
        items.append((now, 0, "step", (key, sends)))
        if key is not None:
            block = key[1], key[2]
            need[block] -= 1
            if need[block] == 0:
                complete[block] = now
                items.append((now, 1, "share", block))
    complete[0, 0] = 0.0
    items.append((0.0, 1, "share", (0, 0)))
    items.append((0.0, 2, "prepare", None))
    done = {}
    for block, now in sorted(complete.items(), key=lambda item: item[1]):
        items.append((now + 2.0, 3, "multiply", block))
        done.setdefault(block[0], []).append((now + 2.0, block))
    for dx, times in done.items():
        last = max(times)[0]
        items.append((last, 4, "scatter", dx))
        items.append((last + 10.0, 5, "store", dx))
    for stage in range(5):
        items.append((4.0 + 5.0 * stage, 6, "bits", stage))
    items.append((3.0, 6, "weights", None))
    final = max(times for times, *_ in items)
    items.append((max(max(times)[0] for times in done.values()), 4.5, "sum", None))
    items.sort(key=lambda item: (item[0], item[1]))
    return [(kind, what) for _, _, kind, what in items]


def kernel(
    a_ref, ap_ref, b_ref, bp_ref, w_ref, wp_ref,
    out_ref, slot_ref, total_ref,
    bg, ae, acc, rs, wa, bm, tot, iy, info, ta,
    a_sem, move_send, move_recv, piece_send, piece_recv, share_send, share_recv,
    w_send, w_recv, rs_send, rs_recv, info_send, info_recv, sum_send, sum_recv,
):
    row, y = lax.axis_index("row"), lax.axis_index("col")
    c = lax.rem(row, 2)
    z = lax.rem(row // 2, NZ)
    x = row // (2 * NZ)

    def device(dx=0, dy=0, dz=0, dc=0):
        xx, zz = lax.rem(x + dx + NX, NX), lax.rem(z + dz + NZ, NZ)
        return ((xx * NZ + zz) * 2 + lax.rem(c + dc, 2), lax.rem(y + dy + NY, NY))

    def place(xx, yy):
        return ((xx * NZ + z) * 2 + c, yy)

    def remote(src, dst, send, recv, to):
        return pltpu.make_async_remote_copy(
            src_ref=src, dst_ref=dst, send_sem=send, recv_sem=recv,
            device_id=to, device_id_type=MESH,
        )

    sent = []

    def go(*args):
        copy = remote(*args)
        copy.start()
        sent.append(copy)

    barrier = pltpu.get_barrier_semaphore()

    def greet(to):
        pl.semaphore_signal(barrier, inc=1, device_id=to, device_id_type=MESH)

    loads = []
    for k in range(NZ):
        load = pltpu.make_async_copy(
            a_ref.at[:, pl.ds(k * 2 * TILE, 2 * TILE)], ae.at[k], a_sem.at[k]
        )
        load.start()
        loads.append(load)
    for d in range(1, NY):
        greet(device(dy=d))
    for d in range(1, NX):
        greet(device(dx=d))
    for d in range(1, NZ):
        greet(device(dz=d))
    greet(device(dc=1))
    diagonal = x == y
    for q in range(NX):
        own = diagonal & (x == q)

        @pl.when(jnp.logical_not(own))
        def _():
            greet(place(q, x))
            greet(place(y, q))

    def flag(ref, n):
        return ref[0, n].astype(jnp.float32).astype(jnp.bfloat16)

    for t in range(2):
        cols = pl.ds(t * TILE, TILE)
        bm[:, cols] = b_ref[:, cols] * flag(bp_ref, t)
    for q in range(NX):
        wa[y, q] = w_ref[:, pl.ds(q * 128, 128)] * flag(wp_ref, q // 2)
    lane = lax.broadcasted_iota(jnp.int32, (1, 128), 1)
    bits = jnp.zeros((1, 128), jnp.float32)
    for t in range(16):
        bits = jnp.where(lane == 16 * y + t, ap_ref[0, t].astype(jnp.float32), bits)
    for t in range(2):
        both = wp_ref[0, t] + 2 * bp_ref[0, t]
        bits = jnp.where(lane == 64 + 2 * y + t, both.astype(jnp.float32), bits)
    iy[0] = bits
    pl.semaphore_wait(barrier, 14 + jnp.where(diagonal, 6, 8))

    for q in range(NX):
        own = diagonal & (x == q)
        rows = pl.ds(pl.multiple_of(y * TILE, TILE), TILE)

        @pl.when(jnp.logical_not(own))
        def _():
            remote(
                bm.at[:, pl.ds(q * 128, 128)], bg.at[q, z, c, rows],
                move_send.at[q], move_recv.at[y], place(q, x),
            ).start()

        @pl.when(own)
        def _():
            bg[q, z, c, rows] = bm[:, pl.ds(q * 128, 128)]

    for q in range(NY):
        own = diagonal & (y == q)

        @pl.when(jnp.logical_not(own))
        def _():
            dst = bg.at[x, z, c, pl.ds(q * TILE, TILE)]
            remote(dst, dst, move_send.at[0], move_recv.at[q], place(y, q)).wait_recv()

    def block(dx, dz):
        return lax.rem(x + dx + NX, NX), lax.rem(z + dz + NZ, NZ)

    def piece(key, dx=0, dz=0):
        first, last = span(key)
        xx, zz = block(key[1] + dx, key[2] + dz)
        return bg.at[xx, zz, c, pl.ds(first, last - first)]

    def step(what):
        key, sends = what
        if key is not None:
            n, dst = KEYS[key], piece(key)
            remote(dst, dst, piece_send.at[n], piece_recv.at[n], device(dc=1)).wait_recv()
        for link, out in sends:
            d = 1 if link[1] == "+" else -1
            to = {"dx": d} if link[0] == "x" else {"dz": d}
            ref, n = piece(out, **to), KEYS[out]
            go(ref, ref, piece_send.at[n], piece_recv.at[n], device(**to))

    def share(what):
        n, (xx, zz) = BLOCK_ID[what], block(*what)
        ref = bg.at[xx, zz, c]
        go(ref, ref, share_send.at[n], share_recv.at[n], device(dc=1))

    def prepare(_):
        for k in range(NZ):
            loads[k].wait()
            for t in range(2):
                cols = pl.ds(t * TILE, TILE)
                ae[k, :, cols] = ae[k, :, cols] * flag(ap_ref, 2 * k + t)

    begun = set()

    def multiply(what):
        n, (xx, zz) = BLOCK_ID[what], block(*what)
        ref = bg.at[xx, zz, 1 - c]
        remote(ref, ref, share_send.at[n], share_recv.at[n], device(dc=1)).wait_recv()
        group = GROUP[what[0]]
        fresh = group not in begun
        begun.add(group)

        def pair(p, carry):
            def part(core, t):
                start = pl.multiple_of((2 * p + t) * TILE, TILE)
                return bg[xx, zz, core, pl.ds(start, TILE), :]

            right = jnp.concatenate(
                [jnp.concatenate([part(k, 0), part(k, 1)], axis=1) for k in range(2)], axis=0
            )
            new = jnp.dot(ae[zz], right, preferred_element_type=jnp.float32)
            for t in range(2):
                new_t = new[:, t * 128 : (t + 1) * 128]
                acc[group, 2 * p + t] = new_t if fresh else acc[group, 2 * p + t] + new_t
            return carry

        lax.fori_loop(0, 2, pair, 0)

    def weights(_):
        for d in range(1, NY):
            go(wa.at[y], wa.at[y], w_send.at[d - 1], w_recv.at[d - 1], device(dy=d))

    heard = []

    def scatter(dx):
        group, xx = GROUP[dx], block(dx, 0)[0]
        for d in range(1, NY):
            yb = lax.rem(y + d, NY)
            n = (d - 1) * NX + group
            go(
                acc.at[group, yb], rs.at[d - 1, group],
                rs_send.at[n], rs_recv.at[n], device(dy=d),
            )
        if not heard:
            heard.append(True)
            tot[...] = jnp.zeros_like(tot)
            for d in range(1, NY):
                ref = wa.at[lax.rem(y + NY - d, NY)]
                remote(ref, ref, w_send.at[d - 1], w_recv.at[d - 1], device(dy=d)).wait_recv()

        def one(yb, carry):
            value = acc[group, yb] * wa[yb, xx].astype(jnp.float32)
            tot[...] += jnp.sum(value.reshape(TILE // 8, 8, 128), axis=0)
            return carry

        lax.fori_loop(0, NY, one, 0)

    def store(dx):
        group, xx = GROUP[dx], block(dx, 0)[0]
        value = acc[group, y]
        for d in range(1, NY):
            n = (d - 1) * NX + group
            ref = rs.at[d - 1, group]
            remote(ref, ref, rs_send.at[n], rs_recv.at[n], device(dy=d)).wait_recv()
            value = value + rs[d - 1, group]
        value = value * wa[y, xx].astype(jnp.float32)
        out_ref[:, pl.ds(pl.multiple_of(xx * 128, 128), 128)] = value.astype(jnp.bfloat16)

    def peers(stage):
        return {
            "y": [(d - 1, {"dy": d}) for d in range(1, NY)],
            "c": [(3, {"dc": 1})],
            "x": [(3 + d, {"dx": d}) for d in range(1, NX)],
            "z": [(6 + d, {"dz": d}) for d in range(1, NZ)],
        }[stage]

    def info_refs(stage, to, back):
        s = -1 if back else 0
        if stage == "y":
            n = to["dy"]
            return (iy.at[0], iy.at[n])
        if stage == "c":
            ref = info.at[z, x, lax.rem(c + 1, 2) if back else c]
        elif stage == "x":
            ref = info.at[z, lax.rem(x + s * to["dx"] + NX, NX)]
        else:
            ref = info.at[lax.rem(z + s * to["dz"] + NZ, NZ)]
        return ref, ref

    def bits_stage(stage):
        order = "ycxz"
        if stage > 0:
            for n, to in peers(order[stage - 1]):
                ref = info_refs(order[stage - 1], to, True)[1]
                remote(ref, ref, info_send.at[n], info_recv.at[n], device(dc=1)).wait_recv()
        if stage == 1:
            info[z, x, c] = iy[0] + iy[1] + iy[2] + iy[3]
        if stage < 4:
            for n, to in peers(order[stage]):
                src, dst = info_refs(order[stage], to, False)
                go(src, dst, info_send.at[n], info_recv.at[n], device(**to))
            return
        at = lax.broadcasted_iota(jnp.int32, (64, 128), 0)
        lanes = lax.broadcasted_iota(jnp.int32, (64, 128), 1)
        table = jnp.zeros((64, 128), jnp.float32)
        for i in range(64):
            xi, zi, ci = i // 16, (i // 2) % 8, i % 2
            table = jnp.where(at == i, info[zi, xi, ci], table)
        tail = lanes >= 64
        bp = jnp.where(tail & (table > 1.5), 1.0, 0.0)
        wp = jnp.where(tail, table - 2.0 * bp, 0.0)
        ap = jnp.where(tail, 0.0, table).astype(jnp.bfloat16)
        wide = jnp.concatenate([bp, jnp.zeros_like(bp)], axis=0).astype(jnp.bfloat16)
        link = jnp.dot(ap, wide, preferred_element_type=jnp.float32)
        present = jnp.where(link > 0.5, wp, 0.0)
        left = (
            lax.broadcasted_iota(jnp.int32, (128, 128), 0)
            < lax.broadcasted_iota(jnp.int32, (128, 128), 1)
        )
        marks = present.astype(jnp.bfloat16)
        inside = jnp.dot(marks, jnp.where(left, 1.0, 0.0).astype(jnp.bfloat16),
                         preferred_element_type=jnp.float32)
        mine = at == row
        earlier = jnp.sum(jnp.where(at < row, present, 0.0))
        before = jnp.sum(jnp.where(mine, inside, 0.0), axis=0, keepdims=True) + earlier
        here = jnp.sum(jnp.where(mine, present, 0.0), axis=0, keepdims=True)
        slots = jnp.where(here > 0.5, before, -1.0)
        pick = lambda t: jnp.sum(jnp.where(lane == 64 + 2 * y + t, slots, 0.0), axis=1, keepdims=True)
        slot_ref[...] = jnp.concatenate([pick(0), pick(1)], axis=1)

    def sum_stages(_):
        value = jnp.sum(tot[...], axis=0, keepdims=True)
        at = {"c": (0, 2, c), "y": (2, NY, y), "x": (6, NX, x), "z": (10, NZ, z)}
        for stage in "cyxz":
            base, size, me = at[stage]
            ta[base + me] = value
            for n, to in peers(stage):
                ref = ta.at[base + me]
                go(ref, ref, sum_send.at[n], sum_recv.at[n], device(**to))
            for n, to in peers(stage):
                back = lax.rem(me + size - next(iter(to.values())), size)
                ref = ta.at[base + back]
                remote(ref, ref, sum_send.at[n], sum_recv.at[n], device(dc=1)).wait_recv()
            value = ta[base]
            for k in range(1, size):
                value = value + ta[base + k]
        total_ref[0, 0] = jnp.sum(value) / (TILE * math.sqrt(64 * 8))

    run = {
        "step": step, "share": share, "prepare": prepare, "multiply": multiply,
        "weights": weights, "scatter": scatter, "store": store, "bits": bits_stage,
        "sum": sum_stages,
    }
    for kind, what in program():
        run[kind](what)
    for copy in sent:
        copy.wait_send()
    for q in range(NX):
        own = diagonal & (x == q)

        @pl.when(jnp.logical_not(own))
        def _():
            src = bm.at[:, pl.ds(q * 128, 128)]
            remote(src, src, move_send.at[q], move_recv.at[0], place(q, x)).wait_send()


def on_device(a_values, a_present, b_values, b_present, w_values, w_present):
    vmem = pl.BlockSpec(memory_space=pltpu.VMEM)
    smem = pl.BlockSpec(memory_space=pltpu.SMEM)
    dma = pltpu.SemaphoreType.DMA
    masked, slot, total = pl.pallas_call(
        kernel,
        out_shape=(
            jax.ShapeDtypeStruct((TILE, 512), jnp.bfloat16),
            jax.ShapeDtypeStruct((1, 2), jnp.float32),
            jax.ShapeDtypeStruct((1, 1), jnp.float32),
        ),
        in_specs=[pl.BlockSpec(memory_space=pl.ANY), smem, vmem, smem, vmem, smem],
        out_specs=(vmem, vmem, smem),
        scratch_shapes=[
            pltpu.VMEM((NX, NZ, 2, BLOCK, 128), jnp.bfloat16),
            pltpu.VMEM((NZ, TILE, 2 * TILE), jnp.bfloat16),
            pltpu.VMEM((NX, NY, TILE, 128), jnp.float32),
            pltpu.VMEM((NY - 1, NX, TILE, 128), jnp.float32),
            pltpu.VMEM((NY, NX, TILE, 128), jnp.bfloat16),
            pltpu.VMEM((TILE, 512), jnp.bfloat16),
            pltpu.VMEM((8, 128), jnp.float32),
            pltpu.VMEM((NY, 1, 128), jnp.float32),
            pltpu.VMEM((NZ, NX, 2, 1, 128), jnp.float32),
            pltpu.VMEM((18, 1, 128), jnp.float32),
            dma((NZ,)), dma((NX,)), dma((NY,)),
            dma((len(KEYS),)), dma((len(KEYS),)),
            dma((len(BLOCKS),)), dma((len(BLOCKS),)),
            dma((3,)), dma((3,)), dma((12,)), dma((12,)),
            dma((14,)), dma((14,)), dma((14,)), dma((14,)),
        ],
        compiler_params=pltpu.CompilerParams(
            collective_id=0, has_side_effects=True, vmem_limit_bytes=50 * 2**20
        ),
    )(a_values, a_present, b_values, b_present, w_values, w_present)
    return masked, slot, total.reshape(())


def solution(mesh):
    spec = P("row", "col")
    return jax.shard_map(
        on_device, mesh=mesh, in_specs=(spec,) * 6, out_specs=(spec, spec, P()),
        check_vma=False,
    )
```

time: 235 us -> 106 us (0.45)
  blocking collectives: 153 us -> 0 us
  Pallas kernels: 0 us -> 96 us
  between operations: 29.5 us -> 2.47 us
  matrix products: 14.8 us -> 0 us
  local copies, waits for them, and re-layouts: 17.8 us -> 6.66 us
  starting transfers between devices: 10.8 us -> 0 us
  other arithmetic: 7.43 us -> 0 us
    pallas_call x0 -> x1, Pallas kernels: none -> 96 us  [on_device(): pl.pallas_call(kernel, out_shape=(jax.ShapeDtypeStruct((TILE, 512), jnp.b...]
    unnamed x4 -> x0, blocking collectives: 69.2 us -> none
    all_gather x1 -> x0, blocking collectives: 43.8 us -> none  [on_device(): b_mask = lax.all_gather(b_present, ROW, axis=0, tiled=True)]
    psum x4 -> x0, blocking collectives: 39.9 us -> none  [by_axis(): return functools.reduce(lax.psum, axes, array)]
    dot_general x2 -> x0, matrix products: 14.8 us -> none  [the longest x1 14 us: on_device(): jnp.dot(a_full, b_piece.reshape(count_tiles * tile_size, col_tiles * tile...]
    all_to_all x2 -> x0, starting transfers between devices: 10.8 us -> none  [sent_to_all(): return lax.all_to_all(copies, axis, split_axis=0, concat_axis=0, tiled=True)]
    mul x5 -> x0, other arithmetic: 6.08 us -> none  [expand(): masked_tiles = blocked * present.astype(values.dtype)[:, None, :, None]]
    broadcast_in_dim x2 -> x0, local copies, waits for them, and re-layouts: 4.98 us -> none  [sent_to_all(): copies = jnp.broadcast_to(array, (lax.axis_size(axis), *array.shape))]
  transfers between devices with their start and end apart: 3 -> 0, of which waited for: 0 -> 0; matrix products, arithmetic and copies ran while one was open for 10% -> 0% of each run, Pallas kernels for 0% -> 0%
where the time goes in v1:
time: 106 us; the launch traced here: 105 us
  Pallas kernels  96 us (91%)
  local copies, waits for them, and re-layouts  6.66 us (6%)
  between operations  2.47 us (2%)
    pallas_call x1, Pallas kernels, on_device(): pl.pallas_call(kernel, out_shape=(jax.ShapeDtypeStruct((TILE, 512), jnp.b...  96 us
    unnamed x14, local copies, waits for them, and re-layouts  6.66 us

profile of v1, /device:TPU:1, one launch (start us, length us, event | category | flops | bytes accessed | tf_op | source)
XLA Modules:
  0.0 105.1 jit_solution(7935855499429938866)
XLA Ops:
  0.6 0.0 copy-start
  0.6 1.6 %copy-done = bf16[256,4096]{1,0:T(8,128)(2,1)S(1)} copy-done((bf16[256,4096]{1,0:T(8,128)(2,1)S(1)}, bf16[256,4096]{1,0:T(8,128)(2,1)}, u32[]{:S(2)}) %copy-start) | copy-done | bytes 2097176
  2.2 0.0 copy-start.1
  2.2 0.9 copy-done.1
  3.2 0.0 copy-start.2
  3.2 0.9 copy-done.2
  4.1 0.0 copy-start.3
  4.1 0.7 copy-done.3
  4.8 0.0 copy-start.4
  4.8 0.7 copy-done.4
  5.4 0.0 copy-start.5
  5.4 0.7 copy-done.5
  6.1 96.0 %shard_map.85 = (bf16[256,512]{1,0:T(8,128)(2,1)S(1)}, f32[1,2]{1,0:T(1,128)S(1)}, f32[1,1]{1,0:T(1,128)}) custom-call(bf16[256,4096]{1,0:T(8,128)(2,1)S(1)} %copy-done, s32[1,16]{1,0:T(1,128)S(1)} %copy-done.3, bf16[256,512]{1,0:T(8,128)(2,1)S(1)} %copy-done.1, s32[1,2]{1,0:T(1,128)S(1)} %copy-done.4, bf16[256,512]{1,0:T(8,128)(2,1)S(1)} %copy-done.2, ...), custom_call_target="tpu_custom_call" | custom-call | tf_op jit(solution)/shard_map/pallas_call | solution.py:439
  102.1 0.7 copy.12
  102.8 0.5 copy.13
Async XLA Ops:
  0.6 1.6 %copy-start = (bf16[256,4096]{1,0:T(8,128)(2,1)S(1)}, bf16[256,4096]{1,0:T(8,128)(2,1)}, u32[]{:S(2)}) copy-start(bf16[256,4096]{1,0:T(8,128)(2,1)} %a_ref.1) | copy-start | bytes 6291460
  2.2 0.9 copy-start.1
  3.2 0.9 copy-start.2
  4.1 0.7 copy-start.3
  4.8 0.7 copy-start.4
  5.4 0.7 copy-start.5

commit v2 on v1

v2 whole, which is shorter than its diff:
```python
import heapq
import math

import jax
import jax.numpy as jnp
from jax import lax
from jax.experimental import pallas as pl
from jax.experimental.pallas import tpu as pltpu
from jax.sharding import PartitionSpec as P

MESH = pl.DeviceIdType.MESH
TILE = 256
NX, NZ, NY = 4, 8, 4
LINKS = ("x+", "x-", "z+", "z-")
PIECES = (
    (True, 0, 256, 0),
    (True, 256, 256, 1),
    (True, 768, 128, 3),
    (False, 512, 256, 2),
    (False, 896, 128, 3),
)
BLOCKS = [(dx, dz) for dx in (0, -1, 1, 2) for dz in (0, -1, 1, -2, 2, -3, 3, 4)]
BLOCK_ID = {block: n for n, block in enumerate(BLOCKS)}
GROUP = {0: 0, -1: 1, 1: 2, 2: 3}
KEY_ID = {
    key: n for n, key in enumerate((p, *block) for p in range(len(PIECES)) for block in BLOCKS)
}
LATENCY, RATE, LEAD = 2.8, 46.6e3, 3.0
STEP, ISSUE, MULTIPLY, SHARE = 0.03, 0.02, 0.47, 1.5
READY = (0.0, 0.6, 1.2, 1.8, 1.2)
X_FIRST_RANK = (0, 1, 2)
X_RANK = (1, 2)
BITS = (1.0, 9.0, 17.0, 26.0, 40.0)
SUMS = (0.0, 1.2, 3.8, 5.0, 3.8)


def program():
    free = dict.fromkeys(LINKS + ("y+", "y-"), 0.0)
    waiting = {link: [] for link in LINKS}
    inbox, ready, items, count = [], [], [], [0]
    missing = {block: len(PIECES) for block in BLOCKS}
    left = {dx: NZ for dx in GROUP}

    def push(heap, when, what):
        count[0] += 1
        heapq.heappush(heap, (when, count[0], what))

    def commit(now):
        sends = []
        for link in LINKS:
            while waiting[link] and free[link] - now < LEAD:
                key = heapq.heappop(waiting[link])[2]
                free[link] = max(now, free[link]) + PIECES[key[0]][2] * 256 / RATE
                push(inbox, free[link] + LATENCY, key)
                sends.append((link, key))
        return tuple(sends)

    def along_y(link, now, rows):
        free[link] = max(now, free[link]) + rows * 512 / RATE
        return free[link] + LATENCY

    def along_z(p, dx, dz):
        rank = -1 if PIECES[p][0] else X_FIRST_RANK[abs(dx)]
        if dz == 0:
            push(waiting["z+"], rank, (p, dx, -1))
            push(waiting["z-"], rank, (p, dx, 1))
        elif abs(dz) < 3:
            sign = 1 if dz > 0 else -1
            push(waiting["z-" if dz > 0 else "z+"], rank, (p, dx, dz + sign))
        elif abs(dz) == 3:
            sign = -1 if (p + abs(dx) // 2 + (dx == 1)) % 2 == 0 else 1
            if (dz < 0) == (sign < 0):
                push(waiting["z-" if dz > 0 else "z+"], rank, (p, dx, 4))

    def along_x(p, dx, dz):
        if dx == 0:
            rank = X_RANK[0] if PIECES[p][0] else -1
            push(waiting["x+"], rank, (p, -1, dz))
            push(waiting["x-"], rank, (p, 1, dz))
        elif dx == (-1 if (p + dz) % 2 == 0 else 1):
            rank = X_RANK[1] if PIECES[p][0] else 0
            push(waiting["x+" if dx < 0 else "x-"], rank, (p, 2, dz))

    for p, when in enumerate(READY):
        push(inbox, when, (p, 0, 0))
    for stage, when in enumerate(BITS):
        push(ready, when, ("bits", stage))
    push(ready, 3.0, ("weights", None))
    push(ready, 2.5, ("prepare", None))
    now, stage = 0.0, 0
    while inbox or ready:
        if inbox and inbox[0][0] <= now:
            key = heapq.heappop(inbox)[2]
            p, dx, dz = key
            if PIECES[p][0]:
                if dx == 0:
                    along_z(*key)
                along_x(*key)
            else:
                if dz == 0:
                    along_x(*key)
                along_z(*key)
            now += STEP
            sends = commit(now)
            now += ISSUE * len(sends)
            items.append(("step", (key, sends)))
            block = dx, dz
            missing[block] -= 1
            if missing[block] == 0:
                items.append(("share", block))
                push(ready, now + SHARE, ("multiply", block))
        elif ready and ready[0][0] <= now:
            kind, what = heapq.heappop(ready)[2]
            items.append((kind, what))
            if kind == "multiply":
                now += MULTIPLY
                dx = what[0]
                left[dx] -= 1
                if left[dx] == 0:
                    items.append(("scatter", dx))
                    now += 0.25
                    first = max(along_y("y+", now, 128), along_y("y-", now, 128))
                    along_y("y+", now, 128), along_y("y-", now, 128)
                    push(ready, first, ("add", dx))
                    if not any(left.values()):
                        push(ready, now, ("sum", 0))
            elif kind == "add":
                now += 0.15
                last = max(along_y("y+", now, 128), along_y("y-", now, 128))
                push(ready, last, ("store", what))
            elif kind == "sum" and what < 4:
                push(ready, now + SUMS[what + 1], ("sum", what + 1))
            elif kind == "prepare":
                now += 0.3
            elif kind == "store":
                now += 0.1
            sends = commit(now)
            if sends:
                items.append(("step", (None, sends)))
        else:
            now = min(heap[0][0] for heap in (inbox, ready) if heap)
    program.end = now
    return items


def kernel(
    a_ref, ap_ref, b_ref, bp_ref, w_ref, wp_ref,
    out_ref, slot_ref, total_ref,
    bg, ae, acc, rl, rs, wa, bm, braw, wraw, masked, tot, iy, info, ta, ap, bp, wp,
    a_sem, in_sem, out_sem, move_send, move_recv, piece_send, piece_recv, share_send, share_recv,
    w_send, w_recv, rs_send, rs_recv, info_send, info_recv, sum_send, sum_recv,
):
    row, y = lax.axis_index("row"), lax.axis_index("col")
    c = lax.rem(row, 2)
    z = lax.rem(row // 2, NZ)
    x = row // (2 * NZ)

    def device(dx=0, dy=0, dz=0, dc=0):
        xx, zz = lax.rem(x + dx + NX, NX), lax.rem(z + dz + NZ, NZ)
        return ((xx * NZ + zz) * 2 + lax.rem(c + dc, 2), lax.rem(y + dy + NY, NY))

    def place(xx, yy):
        return ((xx * NZ + z) * 2 + c, yy)

    def remote(src, dst, send, recv, to):
        return pltpu.make_async_remote_copy(
            src_ref=src, dst_ref=dst, send_sem=send, recv_sem=recv,
            device_id=to, device_id_type=MESH,
        )

    def arrive(dst, recv):
        remote(dst, dst, sum_send.at[0], recv, device(dc=1)).wait_recv()

    sent = []

    def go(*args):
        copy = remote(*args)
        copy.start()
        sent.append(copy)

    loads = [
        pltpu.make_async_copy(src, dst, in_sem.at[n])
        for n, (src, dst) in enumerate(
            ((b_ref, braw), (bp_ref, bp), (ap_ref, ap), (wp_ref, wp), (w_ref, wraw))
        )
    ]
    for k in range(NZ):
        loads.append(pltpu.make_async_copy(
            a_ref.at[:, pl.ds(k * 2 * TILE, 2 * TILE)], ae.at[k], a_sem.at[k]
        ))
    for load in loads:
        load.start()
    barrier = pltpu.get_barrier_semaphore()

    def greet(to):
        pl.semaphore_signal(barrier, inc=1, device_id=to, device_id_type=MESH)

    diagonal = x == y
    for d in range(1, NZ):
        greet(device(dz=d))
    for d in range(1, NX):
        greet(device(dx=d))
    for d in range(1, NY):
        greet(device(dy=d))
    greet(device(dc=1))
    for q in range(NX):

        @pl.when(jnp.logical_not(diagonal & (x == q)))
        def _():
            greet(place(q, x))
            greet(place(y, q))

    def flag(ref, n):
        return ref[0, n].astype(jnp.float32).astype(jnp.bfloat16)

    for load in loads[:2]:
        load.wait()
    for q in range(NX):
        bm[q] = braw[:, pl.ds(q * 128, 128)] * flag(bp, q // 2)
    for load in loads[2:4]:
        load.wait()
    lane = lax.broadcasted_iota(jnp.int32, (1, 128), 1)
    bits = jnp.zeros((1, 128), jnp.float32)
    for t in range(16):
        bits = jnp.where(lane == 16 * y + t, ap[0, t].astype(jnp.float32), bits)
    for t in range(2):
        both = wp[0, t] + 2 * bp[0, t]
        bits = jnp.where(lane == 64 + 2 * y + t, both.astype(jnp.float32), bits)
    iy[0] = bits
    pl.semaphore_wait(barrier, 14 + jnp.where(diagonal, 6, 8))

    mine = lax.rem(y - x + NY, NY)
    rows = pl.ds(pl.multiple_of(mine * TILE, TILE), TILE)

    def move(d):
        q = lax.rem(x + d, NX)
        return remote(
            bm.at[q], bg.at[q, z, c, rows], move_send.at[d], move_recv.at[mine], place(q, x)
        )

    for d in (2, 1, 3):
        move(d).start()

    @pl.when(jnp.logical_not(diagonal))
    def _():
        move(0).start()

    @pl.when(diagonal)
    def _():
        bg[x, z, c, rows] = bm[x]

    landed = set()

    def land(j):
        if j in landed:
            return
        landed.add(j)
        dst = bg.at[x, z, c, pl.ds(j * TILE, TILE)]
        if j > 0:
            arrive(dst, move_recv.at[j])
            return

        @pl.when(jnp.logical_not(diagonal))
        def _():
            arrive(dst, move_recv.at[0])

    def block(dx, dz):
        return lax.rem(x + dx + NX, NX), lax.rem(z + dz + NZ, NZ)

    def piece(key, dx=0, dz=0):
        _, first, size, _ = PIECES[key[0]]
        xx, zz = block(key[1] + dx, key[2] + dz)
        return bg.at[xx, zz, c, pl.ds(first, size)]

    def step(what):
        key, sends = what
        if key is not None:
            if key[1:] == (0, 0):
                land(PIECES[key[0]][3])
            else:
                arrive(piece(key), piece_recv.at[KEY_ID[key]])
        for link, out in sends:
            d = 1 if link[1] == "+" else -1
            to = {"dx": d} if link[0] == "x" else {"dz": d}
            ref, n = piece(out, **to), KEY_ID[out]
            go(ref, ref, piece_send.at[n], piece_recv.at[n], device(**to))

    def share(what):
        n, (xx, zz) = BLOCK_ID[what], block(*what)
        ref = bg.at[xx, zz, c]
        go(ref, ref, share_send.at[n], share_recv.at[n], device(dc=1))

    def prepare(_):
        for load in loads[4:]:
            load.wait()
        for q in range(NX):
            wa[0, q] = wraw[:, pl.ds(q * 128, 128)] * flag(wp, q // 2)
        for k in range(NZ):
            for t in range(2):
                cols = pl.ds(t * TILE, TILE)
                ae[k, :, cols] = ae[k, :, cols] * flag(ap, 2 * k + t)

    begun = set()

    def multiply(what):
        n, (xx, zz) = BLOCK_ID[what], block(*what)
        arrive(bg.at[xx, zz, 1 - c], share_recv.at[n])
        group = GROUP[what[0]]
        fresh = group not in begun
        begun.add(group)

        def pair(p, carry):
            def part(core, t):
                start = pl.multiple_of((2 * p + t) * TILE, TILE)
                return bg[xx, zz, core, pl.ds(start, TILE), :]

            right = jnp.concatenate(
                [jnp.concatenate([part(k, 0), part(k, 1)], axis=1) for k in range(2)], axis=0
            )
            new = jnp.dot(ae[zz], right, preferred_element_type=jnp.float32)
            for t in range(2):
                new_t = new[:, t * 128 : (t + 1) * 128]
                acc[group, 2 * p + t] = new_t if fresh else acc[group, 2 * p + t] + new_t
            return carry

        lax.fori_loop(0, 2, pair, 0)

    def weights(_):
        for d in range(1, NY):
            go(wa.at[0], wa.at[NY - d], w_send.at[d - 1], w_recv.at[d - 1], device(dy=d))

    heard = []
    half = (pl.ds(0, 128), pl.ds(128, 128))

    late = []

    def rs_go(src, dst, n, d):
        copy = remote(src, dst, rs_send.at[n], rs_recv.at[n], device(dy=d))
        copy.start()
        late.append(copy)

    def scatter(dx):
        group, xx = GROUP[dx], block(dx, 0)[0]
        base = 6 * group
        rs_go(acc.at[group, 2, half[0]], rl.at[0, group], base, 1)
        rs_go(acc.at[group, 2, half[1]], rl.at[1, group], base + 1, -1)
        rs_go(acc.at[group, 1, half[1]], rs.at[0, group, half[1]], base + 2, 1)
        rs_go(acc.at[group, 3, half[0]], rs.at[1, group, half[0]], base + 3, -1)
        if not heard:
            heard.append(True)
            tot[...] = jnp.zeros_like(tot)
            for d in range(1, NY):
                arrive(wa.at[NY - d], w_recv.at[d - 1])

        def one(j, carry):
            value = acc[group, j] * wa[j, xx].astype(jnp.float32)
            tot[...] += jnp.sum(value.reshape(TILE // 8, 8, 128), axis=0)
            return carry

        lax.fori_loop(0, NY, one, 0)

    def add(dx):
        group = GROUP[dx]
        base = 6 * group
        arrive(rl.at[0, group], rs_recv.at[base])
        acc[group, 1, half[0]] += rl[0, group]
        rs_go(acc.at[group, 1, half[0]], rs.at[0, group, half[0]], base + 4, 1)
        arrive(rl.at[1, group], rs_recv.at[base + 1])
        acc[group, 3, half[1]] += rl[1, group]
        rs_go(acc.at[group, 3, half[1]], rs.at[1, group, half[1]], base + 5, -1)

    stores = []

    def store(dx):
        group, xx = GROUP[dx], block(dx, 0)[0]
        base = 6 * group
        for n, (side, part) in ((2, (0, 1)), (3, (1, 0)), (4, (0, 0)), (5, (1, 1))):
            arrive(rs.at[side, group, half[part]], rs_recv.at[base + n])
        value = acc[group, 0] + rs[0, group] + rs[1, group]
        value = value * wa[0, xx].astype(jnp.float32)
        masked[group] = value.astype(jnp.bfloat16)
        cols = pl.ds(pl.multiple_of(xx * 128, 128), 128)
        copy = pltpu.make_async_copy(masked.at[group], out_ref.at[:, cols], out_sem.at[group])
        copy.start()
        stores.append(copy)

    PEERS = {
        "y": [(d - 1, {"dy": d}) for d in range(1, NY)],
        "c": [(3, {"dc": 1})],
        "x": [(3 + d, {"dx": d}) for d in range(1, NX)],
        "z": [(6 + d, {"dz": d}) for d in range(1, NZ)],
    }

    def info_refs(stage, to, back):
        s = -1 if back else 0
        if stage == "y":
            return (iy.at[0], iy.at[to["dy"]])
        if stage == "c":
            ref = info.at[z, x, lax.rem(c + 1, 2) if back else c]
        elif stage == "x":
            ref = info.at[z, lax.rem(x + s * to["dx"] + NX, NX)]
        else:
            ref = info.at[lax.rem(z + s * to["dz"] + NZ, NZ)]
        return ref, ref

    def bits_stage(stage):
        order = "ycxz"
        if stage > 0:
            for n, to in PEERS[order[stage - 1]]:
                arrive(info_refs(order[stage - 1], to, True)[1], info_recv.at[n])
        if stage == 1:
            info[z, x, c] = iy[0] + iy[1] + iy[2] + iy[3]
        if stage < 4:
            for n, to in PEERS[order[stage]]:
                src, dst = info_refs(order[stage], to, False)
                go(src, dst, info_send.at[n], info_recv.at[n], device(**to))
            return
        at = lax.broadcasted_iota(jnp.int32, (64, 128), 0)
        lanes = lax.broadcasted_iota(jnp.int32, (64, 128), 1)
        table = jnp.zeros((64, 128), jnp.float32)
        for i in range(64):
            xi, zi, ci = i // 16, (i // 2) % 8, i % 2
            table = jnp.where(at == i, info[zi, xi, ci], table)
        tail = lanes >= 64
        bp = jnp.where(tail & (table > 1.5), 1.0, 0.0)
        wp = jnp.where(tail, table - 2.0 * bp, 0.0)
        ap = jnp.where(tail, 0.0, table).astype(jnp.bfloat16)
        wide = jnp.concatenate([bp, jnp.zeros_like(bp)], axis=0).astype(jnp.bfloat16)
        link = jnp.dot(ap, wide, preferred_element_type=jnp.float32)
        present = jnp.where(link > 0.5, wp, 0.0)
        left = (
            lax.broadcasted_iota(jnp.int32, (128, 128), 0)
            < lax.broadcasted_iota(jnp.int32, (128, 128), 1)
        )
        marks = present.astype(jnp.bfloat16)
        inside = jnp.dot(marks, jnp.where(left, 1.0, 0.0).astype(jnp.bfloat16),
                         preferred_element_type=jnp.float32)
        own = at == row
        earlier = jnp.sum(jnp.where(at < row, present, 0.0))
        before = jnp.sum(jnp.where(own, inside, 0.0), axis=0, keepdims=True) + earlier
        here = jnp.sum(jnp.where(own, present, 0.0), axis=0, keepdims=True)
        slots = jnp.where(here > 0.5, before, -1.0)
        for t in range(2):
            slot_ref[0, t] = jnp.sum(jnp.where(lane == 64 + 2 * y + t, slots, 0.0))

    SUM_AT = {"c": (0, 2, c), "y": (2, NY, y), "x": (6, NX, x), "z": (10, NZ, z)}
    SUM_ORDER = "cxzy"

    def sum_stage(k):
        if k == 0:
            value = jnp.sum(tot[...], axis=0, keepdims=True)
        else:
            base, size, me = SUM_AT[SUM_ORDER[k - 1]]
            for n, to in PEERS[SUM_ORDER[k - 1]]:
                back = lax.rem(me + size - next(iter(to.values())), size)
                arrive(ta.at[base + back], sum_recv.at[n])
            value = ta[base]
            for i in range(1, size):
                value = value + ta[base + i]
        if k == 4:
            total_ref[0, 0] = jnp.sum(value) / (TILE * math.sqrt(64 * 8))
            return
        base, _, me = SUM_AT[SUM_ORDER[k]]
        ta[base + me] = value
        for n, to in PEERS[SUM_ORDER[k]]:
            ref = ta.at[base + me]
            go(ref, ref, sum_send.at[n], sum_recv.at[n], device(**to))
        if k == 1:
            finish()

    def finish():
        while sent:
            sent.pop(0).wait_send()

    run = {
        "step": step, "share": share, "prepare": prepare, "multiply": multiply,
        "weights": weights, "scatter": scatter, "add": add, "store": store,
        "bits": bits_stage, "sum": sum_stage,
    }
    for kind, what in program():
        run[kind](what)
    finish()
    for copy in late:
        copy.wait_send()
    for copy in stores:
        copy.wait()
    for d in (1, 2, 3):
        move(d).wait_send()

    @pl.when(jnp.logical_not(diagonal))
    def _():
        move(0).wait_send()


def on_device(a_values, a_present, b_values, b_present, w_values, w_present):
    hbm = pl.BlockSpec(memory_space=pltpu.HBM)
    smem = pl.BlockSpec(memory_space=pltpu.SMEM)
    dma = pltpu.SemaphoreType.DMA
    bf16, f32, i32 = jnp.bfloat16, jnp.float32, jnp.int32
    masked, slot, total = pl.pallas_call(
        kernel,
        out_shape=(
            jax.ShapeDtypeStruct((TILE, 512), bf16),
            jax.ShapeDtypeStruct((1, 2), f32),
            jax.ShapeDtypeStruct((1, 1), f32),
        ),
        in_specs=[hbm] * 6,
        out_specs=(hbm, smem, smem),
        scratch_shapes=[
            pltpu.VMEM((NX, NZ, 2, 1024, 128), bf16),
            pltpu.VMEM((NZ, TILE, 2 * TILE), bf16),
            pltpu.VMEM((NX, NY, TILE, 128), f32),
            pltpu.VMEM((2, NX, 128, 128), f32),
            pltpu.VMEM((2, NX, TILE, 128), f32),
            pltpu.VMEM((NY, NX, TILE, 128), bf16),
            pltpu.VMEM((NX, TILE, 128), bf16),
            pltpu.VMEM((TILE, 512), bf16),
            pltpu.VMEM((TILE, 512), bf16),
            pltpu.VMEM((NX, TILE, 128), bf16),
            pltpu.VMEM((8, 128), f32),
            pltpu.VMEM((NY, 1, 128), f32),
            pltpu.VMEM((NZ, NX, 2, 1, 128), f32),
            pltpu.VMEM((18, 1, 128), f32),
            pltpu.SMEM((1, 16), i32),
            pltpu.SMEM((1, 2), i32),
            pltpu.SMEM((1, 2), i32),
            dma((NZ,)), dma((5,)), dma((NX,)), dma((NX,)), dma((NY,)),
            dma((len(KEY_ID),)), dma((len(KEY_ID),)),
            dma((len(BLOCKS),)), dma((len(BLOCKS),)),
            dma((3,)), dma((3,)), dma((24,)), dma((24,)),
            dma((14,)), dma((14,)), dma((14,)), dma((14,)),
        ],
        compiler_params=pltpu.CompilerParams(
            collective_id=0, has_side_effects=True, vmem_limit_bytes=60 * 2**20
        ),
    )(a_values, a_present, b_values, b_present, w_values, w_present)
    return masked, slot, total.reshape(())


def solution(mesh):
    spec = P("row", "col")
    return jax.shard_map(
        on_device, mesh=mesh, in_specs=(spec,) * 6, out_specs=(spec, spec, P()),
        check_vma=False,
    )
```

time: 106 us -> 88 us (0.83)
  Pallas kernels: 96 us -> 82.2 us
  local copies, waits for them, and re-layouts: 6.66 us -> 2.8 us
    pallas_call x1, Pallas kernels: 96 us -> 82.2 us  [on_device(): pl.pallas_call(kernel, out_shape=(jax.ShapeDtypeStruct((TILE, 512), bf16)...]
    unnamed x14 -> x2, local copies, waits for them, and re-layouts: 6.66 us -> 2.8 us
where the time goes in v2:
time: 88 us; the launch traced here: 87.3 us
  Pallas kernels  82.2 us (93%)
  local copies, waits for them, and re-layouts  2.8 us (3%)
  between operations  2.32 us (3%)
    pallas_call x1, Pallas kernels, on_device(): pl.pallas_call(kernel, out_shape=(jax.ShapeDtypeStruct((TILE, 512), bf16)...  82.2 us
    unnamed x2, local copies, waits for them, and re-layouts  2.8 us

profile of v2, /device:TPU:1, one launch (start us, length us, event | category | flops | bytes accessed | tf_op | source)
XLA Modules:
  0.0 87.3 jit_solution(12485819138798718406)
XLA Ops:
  0.6 82.2 %shard_map.85 = (bf16[256,512]{1,0:T(8,128)(2,1)}, f32[1,2]{1,0:T(1,128)}, f32[1,1]{1,0:T(1,128)}) custom-call(bf16[256,4096]{1,0:T(8,128)(2,1)} %a_ref.1, s32[1,16]{1,0:T(1,128)} %ap_ref.1, bf16[256,512]{1,0:T(8,128)(2,1)} %b_ref.1, s32[1,2]{1,0:T(1,128)} %bp_ref.1, bf16[256,512]{1,0:T(8,128)(2,1)} %w_ref.1, s32[1,2]{1,0:T(1,128)} %wp_ref.1), custom_call_target="tpu_custom_call" | custom-call | tf_op jit(solution)/shard_map/pallas_call | solution.py:500
  82.8 1.7 %copy.12 = bf16[256,512]{1,0:T(8,128)(2,1)} copy(bf16[256,512]{1,0:T(8,128)(2,1)} %get-tuple-element.12) | data formatting | bytes 524288
  84.5 1.1 %copy.13 = f32[1,2]{1,0:T(1,128)} copy(f32[1,2]{1,0:T(1,128)} %get-tuple-element.13) | data formatting | bytes 16

commit v3 on v2

--- a/solution.py
+++ b/solution.py
@@ -23,15 +23,16 @@
 BLOCK_ID = {block: n for n, block in enumerate(BLOCKS)}
 GROUP = {0: 0, -1: 1, 1: 2, 2: 3}
 KEY_ID = {
-    key: n for n, key in enumerate((p, *block) for p in range(len(PIECES)) for block in BLOCKS)
+    key: n for n, key in enumerate((p, *block) for p in range(len(PIECES)) for block in BLOCKS[1:])
 }
-LATENCY, RATE, LEAD = 2.8, 46.6e3, 3.0
+MOVED = NX * NZ - 1
+LATENCY, RATE, LEAD = 2.8, 46.6e3, 2.0
 STEP, ISSUE, MULTIPLY, SHARE = 0.03, 0.02, 0.47, 1.5
-READY = (0.0, 0.6, 1.2, 1.8, 1.2)
+READY = (0.0, 0.8, 0.8, 1.2, 0.8)
 X_FIRST_RANK = (0, 1, 2)
 X_RANK = (1, 2)
-BITS = (1.0, 9.0, 17.0, 26.0, 40.0)
-SUMS = (0.0, 1.2, 3.8, 5.0, 3.8)
+BITS = (1.0, 12.0, 30.0)
+SUMS = (0.0, 4.2, 4.2)
 
 
 def program():
@@ -128,7 +129,7 @@
                 now += 0.15
                 last = max(along_y("y+", now, 128), along_y("y-", now, 128))
                 push(ready, last, ("store", what))
-            elif kind == "sum" and what < 4:
+            elif kind == "sum" and what < 2:
                 push(ready, now + SUMS[what + 1], ("sum", what + 1))
             elif kind == "prepare":
                 now += 0.3
@@ -146,9 +147,9 @@
 def kernel(
     a_ref, ap_ref, b_ref, bp_ref, w_ref, wp_ref,
     out_ref, slot_ref, total_ref,
-    bg, ae, acc, rl, rs, wa, bm, braw, wraw, masked, tot, iy, info, ta, ap, bp, wp,
-    a_sem, in_sem, out_sem, move_send, move_recv, piece_send, piece_recv, share_send, share_recv,
-    w_send, w_recv, rs_send, rs_recv, info_send, info_recv, sum_send, sum_recv,
+    bg, ae, acc, rl, rs, wa, bm, braw, wraw, masked, slots_v, tot, ixy, info, ta, ap, bp, wp,
+    a_sem, in_sem, out_sem, move_send, move_recv, bulk_send, piece_recv, share_recv,
+    w_send, w_recv, rs_send, rl_recv, rs_recv, info_send, info_recv, sum_send, sum_recv,
 ):
     row, y = lax.axis_index("row"), lax.axis_index("col")
     c = lax.rem(row, 2)
@@ -169,14 +170,20 @@
         )
 
     def arrive(dst, recv):
-        remote(dst, dst, sum_send.at[0], recv, device(dc=1)).wait_recv()
-
-    sent = []
+        remote(dst, dst, sum_send, recv, device(dc=1)).wait_recv()
+
+    def gone(src, send):
+        remote(src, src, send, sum_recv.at[0], device(dc=1)).wait_send()
 
     def go(*args):
-        copy = remote(*args)
-        copy.start()
-        sent.append(copy)
+        remote(*args).start()
+
+    def at(xx, zz, core, first=0, size=1024):
+        start = ((xx * NZ + zz) * 2 + core) * 1024 + first
+        return pl.ds(pl.multiple_of(start, 16), size)
+
+    ZC = [{"dz": d, "dc": e} for d in range(NZ) for e in range(2)][1:]
+    XY = [{"dx": d, "dy": e} for d in range(NX) for e in range(NY)][1:]
 
     loads = [
         pltpu.make_async_copy(src, dst, in_sem.at[n])
@@ -186,7 +193,7 @@
     ]
     for k in range(NZ):
         loads.append(pltpu.make_async_copy(
-            a_ref.at[:, pl.ds(k * 2 * TILE, 2 * TILE)], ae.at[k], a_sem.at[k]
+            a_ref.at[:, pl.ds(k * 2 * TILE, 2 * TILE)], ae.at[k], a_sem
         ))
     for load in loads:
         load.start()
@@ -195,20 +202,8 @@
     def greet(to):
         pl.semaphore_signal(barrier, inc=1, device_id=to, device_id_type=MESH)
 
-    diagonal = x == y
-    for d in range(1, NZ):
-        greet(device(dz=d))
-    for d in range(1, NX):
-        greet(device(dx=d))
-    for d in range(1, NY):
-        greet(device(dy=d))
-    greet(device(dc=1))
-    for q in range(NX):
-
-        @pl.when(jnp.logical_not(diagonal & (x == q)))
-        def _():
-            greet(place(q, x))
-            greet(place(y, q))
+    for to in ZC + XY:
+        greet(device(**to))
 
     def flag(ref, n):
         return ref[0, n].astype(jnp.float32).astype(jnp.bfloat16)
@@ -226,17 +221,16 @@
     for t in range(2):
         both = wp[0, t] + 2 * bp[0, t]
         bits = jnp.where(lane == 64 + 2 * y + t, both.astype(jnp.float32), bits)
-    iy[0] = bits
-    pl.semaphore_wait(barrier, 14 + jnp.where(diagonal, 6, 8))
-
+    ixy[x * NY + y] = bits
+    pl.semaphore_wait(barrier, len(ZC + XY))
+
+    diagonal = x == y
     mine = lax.rem(y - x + NY, NY)
-    rows = pl.ds(pl.multiple_of(mine * TILE, TILE), TILE)
 
     def move(d):
         q = lax.rem(x + d, NX)
-        return remote(
-            bm.at[q], bg.at[q, z, c, rows], move_send.at[d], move_recv.at[mine], place(q, x)
-        )
+        dst = bg.at[at(q, z, c, mine * TILE, TILE)]
+        return remote(bm.at[q], dst, move_send.at[d], move_recv.at[mine], place(q, x))
 
     for d in (2, 1, 3):
         move(d).start()
@@ -247,7 +241,7 @@
 
     @pl.when(diagonal)
     def _():
-        bg[x, z, c, rows] = bm[x]
+        bg[at(x, z, c, mine * TILE, TILE)] = bm[x]
 
     landed = set()
 
@@ -255,7 +249,7 @@
         if j in landed:
             return
         landed.add(j)
-        dst = bg.at[x, z, c, pl.ds(j * TILE, TILE)]
+        dst = bg.at[at(x, z, c, j * TILE, TILE)]
         if j > 0:
             arrive(dst, move_recv.at[j])
             return
@@ -270,7 +264,7 @@
     def piece(key, dx=0, dz=0):
         _, first, size, _ = PIECES[key[0]]
         xx, zz = block(key[1] + dx, key[2] + dz)
-        return bg.at[xx, zz, c, pl.ds(first, size)]
+        return bg.at[at(xx, zz, c, first, size)]
 
     def step(what):
         key, sends = what
@@ -283,16 +277,16 @@
             d = 1 if link[1] == "+" else -1
             to = {"dx": d} if link[0] == "x" else {"dz": d}
             ref, n = piece(out, **to), KEY_ID[out]
-            go(ref, ref, piece_send.at[n], piece_recv.at[n], device(**to))
+            go(ref, ref, bulk_send, piece_recv.at[n], device(**to))
 
     def share(what):
         n, (xx, zz) = BLOCK_ID[what], block(*what)
-        ref = bg.at[xx, zz, c]
-        go(ref, ref, share_send.at[n], share_recv.at[n], device(dc=1))
+        ref = bg.at[at(xx, zz, c)]
+        go(ref, ref, bulk_send, share_recv.at[n], device(dc=1))
 
     def prepare(_):
-        for load in loads[4:]:
-            load.wait()
+        loads[4].wait()
+        pltpu.make_async_copy(ae, ae, a_sem).wait()
         for q in range(NX):
             wa[0, q] = wraw[:, pl.ds(q * 128, 128)] * flag(wp, q // 2)
         for k in range(NZ):
@@ -304,15 +298,14 @@
 
     def multiply(what):
         n, (xx, zz) = BLOCK_ID[what], block(*what)
-        arrive(bg.at[xx, zz, 1 - c], share_recv.at[n])
+        arrive(bg.at[at(xx, zz, 1 - c)], share_recv.at[n])
         group = GROUP[what[0]]
         fresh = group not in begun
         begun.add(group)
 
         def pair(p, carry):
             def part(core, t):
-                start = pl.multiple_of((2 * p + t) * TILE, TILE)
-                return bg[xx, zz, core, pl.ds(start, TILE), :]
+                return bg[at(xx, zz, core, (2 * p + t) * TILE, TILE), :]
 
             right = jnp.concatenate(
                 [jnp.concatenate([part(k, 0), part(k, 1)], axis=1) for k in range(2)], axis=0
@@ -327,30 +320,24 @@
 
     def weights(_):
         for d in range(1, NY):
-            go(wa.at[0], wa.at[NY - d], w_send.at[d - 1], w_recv.at[d - 1], device(dy=d))
+            go(wa.at[0], wa.at[NY - d], w_send, w_recv, device(dy=d))
 
     heard = []
     half = (pl.ds(0, 128), pl.ds(128, 128))
 
-    late = []
-
-    def rs_go(src, dst, n, d):
-        copy = remote(src, dst, rs_send.at[n], rs_recv.at[n], device(dy=d))
-        copy.start()
-        late.append(copy)
-
     def scatter(dx):
         group, xx = GROUP[dx], block(dx, 0)[0]
-        base = 6 * group
-        rs_go(acc.at[group, 2, half[0]], rl.at[0, group], base, 1)
-        rs_go(acc.at[group, 2, half[1]], rl.at[1, group], base + 1, -1)
-        rs_go(acc.at[group, 1, half[1]], rs.at[0, group, half[1]], base + 2, 1)
-        rs_go(acc.at[group, 3, half[0]], rs.at[1, group, half[0]], base + 3, -1)
+        for d, src, dst, recv in (
+            (1, acc.at[group, 2, half[0]], rl.at[group, 0], rl_recv),
+            (-1, acc.at[group, 2, half[1]], rl.at[group, 1], rl_recv),
+            (1, acc.at[group, 1, half[1]], rs.at[group, 0, half[1]], rs_recv),
+            (-1, acc.at[group, 3, half[0]], rs.at[group, 1, half[0]], rs_recv),
+        ):
+            go(src, dst, rs_send, recv.at[group], device(dy=d))
         if not heard:
             heard.append(True)
             tot[...] = jnp.zeros_like(tot)
-            for d in range(1, NY):
-                arrive(wa.at[NY - d], w_recv.at[d - 1])
+            arrive(wa.at[pl.ds(1, NY - 1)], w_recv)
 
         def one(j, carry):
             value = acc[group, j] * wa[j, xx].astype(jnp.float32)
@@ -361,66 +348,51 @@
 
     def add(dx):
         group = GROUP[dx]
-        base = 6 * group
-        arrive(rl.at[0, group], rs_recv.at[base])
-        acc[group, 1, half[0]] += rl[0, group]
-        rs_go(acc.at[group, 1, half[0]], rs.at[0, group, half[0]], base + 4, 1)
-        arrive(rl.at[1, group], rs_recv.at[base + 1])
-        acc[group, 3, half[1]] += rl[1, group]
-        rs_go(acc.at[group, 3, half[1]], rs.at[1, group, half[1]], base + 5, -1)
-
-    stores = []
+        arrive(rl.at[group], rl_recv.at[group])
+        acc[group, 1, half[0]] += rl[group, 0]
+        acc[group, 3, half[1]] += rl[group, 1]
+        for d, tile, side, part in ((1, 1, 0, 0), (-1, 3, 1, 1)):
+            src, dst = acc.at[group, tile, half[part]], rs.at[group, side, half[part]]
+            go(src, dst, rs_send, rs_recv.at[group], device(dy=d))
+
+    outs = []
+
+    def put(src, dst, n):
+        copy = pltpu.make_async_copy(src, dst, out_sem.at[n])
+        copy.start()
+        outs.append(copy)
 
     def store(dx):
         group, xx = GROUP[dx], block(dx, 0)[0]
-        base = 6 * group
-        for n, (side, part) in ((2, (0, 1)), (3, (1, 0)), (4, (0, 0)), (5, (1, 1))):
-            arrive(rs.at[side, group, half[part]], rs_recv.at[base + n])
-        value = acc[group, 0] + rs[0, group] + rs[1, group]
+        arrive(rs.at[group], rs_recv.at[group])
+        value = acc[group, 0] + rs[group, 0] + rs[group, 1]
         value = value * wa[0, xx].astype(jnp.float32)
+        cols = pl.ds(pl.multiple_of(xx * 128, 128), 128)
         masked[group] = value.astype(jnp.bfloat16)
-        cols = pl.ds(pl.multiple_of(xx * 128, 128), 128)
-        copy = pltpu.make_async_copy(masked.at[group], out_ref.at[:, cols], out_sem.at[group])
-        copy.start()
-        stores.append(copy)
-
-    PEERS = {
-        "y": [(d - 1, {"dy": d}) for d in range(1, NY)],
-        "c": [(3, {"dc": 1})],
-        "x": [(3 + d, {"dx": d}) for d in range(1, NX)],
-        "z": [(6 + d, {"dz": d}) for d in range(1, NZ)],
-    }
-
-    def info_refs(stage, to, back):
-        s = -1 if back else 0
-        if stage == "y":
-            return (iy.at[0], iy.at[to["dy"]])
-        if stage == "c":
-            ref = info.at[z, x, lax.rem(c + 1, 2) if back else c]
-        elif stage == "x":
-            ref = info.at[z, lax.rem(x + s * to["dx"] + NX, NX)]
-        else:
-            ref = info.at[lax.rem(z + s * to["dz"] + NZ, NZ)]
-        return ref, ref
+        put(masked.at[group], out_ref.at[:, cols], group)
 
     def bits_stage(stage):
-        order = "ycxz"
-        if stage > 0:
-            for n, to in PEERS[order[stage - 1]]:
-                arrive(info_refs(order[stage - 1], to, True)[1], info_recv.at[n])
+        if stage == 0:
+            for to in XY:
+                ref = ixy.at[x * NY + y]
+                go(ref, ref, info_send.at[0], info_recv.at[0], device(**to))
+            return
         if stage == 1:
-            info[z, x, c] = iy[0] + iy[1] + iy[2] + iy[3]
-        if stage < 4:
-            for n, to in PEERS[order[stage]]:
-                src, dst = info_refs(order[stage], to, False)
-                go(src, dst, info_send.at[n], info_recv.at[n], device(**to))
+            arrive(ixy.at[pl.ds(0, len(XY))], info_recv.at[0])
+            rows = pl.ds((z * 2 + c) * NX, NX)
+            for k in range(NX):
+                line = [ixy[k * NY + n] for n in range(NY)]
+                info[(z * 2 + c) * NX + k] = line[0] + line[1] + line[2] + line[3]
+            for to in ZC:
+                go(info.at[rows], info.at[rows], info_send.at[1], info_recv.at[1], device(**to))
             return
-        at = lax.broadcasted_iota(jnp.int32, (64, 128), 0)
+        arrive(info.at[pl.ds(0, NX * len(ZC))], info_recv.at[1])
+        line = lax.broadcasted_iota(jnp.int32, (64, 128), 0)
         lanes = lax.broadcasted_iota(jnp.int32, (64, 128), 1)
         table = jnp.zeros((64, 128), jnp.float32)
         for i in range(64):
             xi, zi, ci = i // 16, (i // 2) % 8, i % 2
-            table = jnp.where(at == i, info[zi, xi, ci], table)
+            table = jnp.where(line == i, info[(zi * 2 + ci) * NX + xi], table)
         tail = lanes >= 64
         bp = jnp.where(tail & (table > 1.5), 1.0, 0.0)
         wp = jnp.where(tail, table - 2.0 * bp, 0.0)
@@ -435,42 +407,33 @@
         marks = present.astype(jnp.bfloat16)
         inside = jnp.dot(marks, jnp.where(left, 1.0, 0.0).astype(jnp.bfloat16),
                          preferred_element_type=jnp.float32)
-        own = at == row
-        earlier = jnp.sum(jnp.where(at < row, present, 0.0))
+        own = line == row
+        earlier = jnp.sum(jnp.where(line < row, present, 0.0))
         before = jnp.sum(jnp.where(own, inside, 0.0), axis=0, keepdims=True) + earlier
         here = jnp.sum(jnp.where(own, present, 0.0), axis=0, keepdims=True)
         slots = jnp.where(here > 0.5, before, -1.0)
         for t in range(2):
-            slot_ref[0, t] = jnp.sum(jnp.where(lane == 64 + 2 * y + t, slots, 0.0))
-
-    SUM_AT = {"c": (0, 2, c), "y": (2, NY, y), "x": (6, NX, x), "z": (10, NZ, z)}
-    SUM_ORDER = "cxzy"
+            here = jnp.where(lane == 64 + 2 * y + t, slots, 0.0)
+            slots_v[:, pl.ds(t, 1)] = jnp.sum(here, axis=1, keepdims=True)
+        put(slots_v, slot_ref, 4)
 
     def sum_stage(k):
         if k == 0:
             value = jnp.sum(tot[...], axis=0, keepdims=True)
+            first, size, mine, peers = 0, 16, z * 2 + c, ZC
         else:
-            base, size, me = SUM_AT[SUM_ORDER[k - 1]]
-            for n, to in PEERS[SUM_ORDER[k - 1]]:
-                back = lax.rem(me + size - next(iter(to.values())), size)
-                arrive(ta.at[base + back], sum_recv.at[n])
-            value = ta[base]
-            for i in range(1, size):
-                value = value + ta[base + i]
-        if k == 4:
+            arrive(ta.at[pl.ds(16 * (k - 1), 15)], sum_recv.at[k - 1])
+            value = ta[16 * (k - 1)]
+            for n in range(1, 16):
+                value = value + ta[16 * (k - 1) + n]
+            first, size, mine, peers = 16, 16, x * NY + y, XY
+        if k == 2:
             total_ref[0, 0] = jnp.sum(value) / (TILE * math.sqrt(64 * 8))
             return
-        base, _, me = SUM_AT[SUM_ORDER[k]]
-        ta[base + me] = value
-        for n, to in PEERS[SUM_ORDER[k]]:
-            ref = ta.at[base + me]
-            go(ref, ref, sum_send.at[n], sum_recv.at[n], device(**to))
-        if k == 1:
-            finish()
-
-    def finish():
-        while sent:
-            sent.pop(0).wait_send()
+        ta[first + mine] = value
+        for to in peers:
+            ref = ta.at[first + mine]
+            go(ref, ref, sum_send, sum_recv.at[k], device(**to))
 
     run = {
         "step": step, "share": share, "prepare": prepare, "multiply": multiply,
@@ -479,10 +442,13 @@
     }
     for kind, what in program():
         run[kind](what)
-    finish()
-    for copy in late:
-        copy.wait_send()
-    for copy in stores:
+    gone(bg.at[pl.ds(0, (2 * MOVED + 1) * 1024)], bulk_send)
+    gone(acc.at[pl.ds(0, 3)], rs_send)
+    gone(wa.at[pl.ds(0, 3)], w_send)
+    gone(ixy.at[pl.ds(0, 15)], info_send.at[0])
+    gone(info.at[pl.ds(0, 60)], info_send.at[1])
+    gone(ta.at[pl.ds(0, 30)], sum_send)
+    for copy in outs:
         copy.wait()
     for d in (1, 2, 3):
         move(d).wait_send()
@@ -505,30 +471,30 @@
             jax.ShapeDtypeStruct((1, 1), f32),
         ),
         in_specs=[hbm] * 6,
-        out_specs=(hbm, smem, smem),
+        out_specs=(hbm, hbm, smem),
         scratch_shapes=[
-            pltpu.VMEM((NX, NZ, 2, 1024, 128), bf16),
+            pltpu.VMEM((NX * NZ * 2 * 1024, 128), bf16),
             pltpu.VMEM((NZ, TILE, 2 * TILE), bf16),
             pltpu.VMEM((NX, NY, TILE, 128), f32),
-            pltpu.VMEM((2, NX, 128, 128), f32),
-            pltpu.VMEM((2, NX, TILE, 128), f32),
+            pltpu.VMEM((NX, 2, 128, 128), f32),
+            pltpu.VMEM((NX, 2, TILE, 128), f32),
             pltpu.VMEM((NY, NX, TILE, 128), bf16),
             pltpu.VMEM((NX, TILE, 128), bf16),
             pltpu.VMEM((TILE, 512), bf16),
             pltpu.VMEM((TILE, 512), bf16),
             pltpu.VMEM((NX, TILE, 128), bf16),
+            pltpu.VMEM((1, 2), f32),
             pltpu.VMEM((8, 128), f32),
-            pltpu.VMEM((NY, 1, 128), f32),
-            pltpu.VMEM((NZ, NX, 2, 1, 128), f32),
-            pltpu.VMEM((18, 1, 128), f32),
+            pltpu.VMEM((NX * NY, 1, 128), f32),
+            pltpu.VMEM((64, 1, 128), f32),
+            pltpu.VMEM((32, 1, 128), f32),
             pltpu.SMEM((1, 16), i32),
             pltpu.SMEM((1, 2), i32),
             pltpu.SMEM((1, 2), i32),
-            dma((NZ,)), dma((5,)), dma((NX,)), dma((NX,)), dma((NY,)),
-            dma((len(KEY_ID),)), dma((len(KEY_ID),)),
-            dma((len(BLOCKS),)), dma((len(BLOCKS),)),
-            dma((3,)), dma((3,)), dma((24,)), dma((24,)),
-            dma((14,)), dma((14,)), dma((14,)), dma((14,)),
+            dma, dma((5,)), dma((5,)), dma((NX,)), dma((NY,)),
+            dma, dma((len(KEY_ID),)), dma((len(BLOCKS),)),
+            dma, dma, dma, dma((NX,)), dma((NX,)),
+            dma((2,)), dma((2,)), dma, dma((2,)),
         ],
         compiler_params=pltpu.CompilerParams(
             collective_id=0, has_side_effects=True, vmem_limit_bytes=60 * 2**20

time: 88 us -> 83.7 us (0.951)
  Pallas kernels: 82.2 us -> 78.4 us
    pallas_call x1, Pallas kernels: 82.2 us -> 78.4 us  [on_device(): pl.pallas_call(kernel, out_shape=(jax.ShapeDtypeStruct((TILE, 512), bf16)...]
where the time goes in v3:
time: 83.7 us; the launch traced here: 83.5 us
  Pallas kernels  78.4 us (94%)
  local copies, waits for them, and re-layouts  2.8 us (3%)
  between operations  2.32 us (3%)
    pallas_call x1, Pallas kernels, on_device(): pl.pallas_call(kernel, out_shape=(jax.ShapeDtypeStruct((TILE, 512), bf16)...  78.4 us
    unnamed x2, local copies, waits for them, and re-layouts  2.8 us

profile of v3, /device:TPU:1, one launch (start us, length us, event | category | flops | bytes accessed | tf_op | source)
XLA Modules:
  0.0 83.5 jit_solution(14217140796575876535)
XLA Ops:
  0.6 78.4 %shard_map.85 = (bf16[256,512]{1,0:T(8,128)(2,1)}, f32[1,2]{1,0:T(1,128)}, f32[1,1]{1,0:T(1,128)}) custom-call(bf16[256,4096]{1,0:T(8,128)(2,1)} %a_ref.1, s32[1,16]{1,0:T(1,128)} %ap_ref.1, bf16[256,512]{1,0:T(8,128)(2,1)} %b_ref.1, s32[1,2]{1,0:T(1,128)} %bp_ref.1, bf16[256,512]{1,0:T(8,128)(2,1)} %w_ref.1, s32[1,2]{1,0:T(1,128)} %wp_ref.1), custom_call_target="tpu_custom_call" | custom-call | tf_op jit(solution)/shard_map/pallas_call | solution.py:466
  79.1 1.7 %copy.12 = bf16[256,512]{1,0:T(8,128)(2,1)} copy(bf16[256,512]{1,0:T(8,128)(2,1)} %get-tuple-element.12) | data formatting | bytes 524288
  80.7 1.1 %copy.13 = f32[1,2]{1,0:T(1,128)} copy(f32[1,2]{1,0:T(1,128)} %get-tuple-element.13) | data formatting | bytes 16

commit v4 on v3

--- a/solution.py
+++ b/solution.py
@@ -13,33 +13,44 @@
 NX, NZ, NY = 4, 8, 4
 LINKS = ("x+", "x-", "z+", "z-")
 PIECES = (
-    (True, 0, 256, 0),
-    (True, 256, 256, 1),
-    (True, 768, 128, 3),
-    (False, 512, 256, 2),
-    (False, 896, 128, 3),
+    ("Z", 0, 256, (0,)),
+    ("Z", 256, 352, (1, 2)),
+    ("X", 608, 416, (2, 3)),
+    ("J", 0, 608, ()),
 )
+JOINED = len(PIECES) - 1
 BLOCKS = [(dx, dz) for dx in (0, -1, 1, 2) for dz in (0, -1, 1, -2, 2, -3, 3, 4)]
 BLOCK_ID = {block: n for n, block in enumerate(BLOCKS)}
 GROUP = {0: 0, -1: 1, 1: 2, 2: 3}
-KEY_ID = {
-    key: n for n, key in enumerate((p, *block) for p in range(len(PIECES)) for block in BLOCKS[1:])
-}
+KEYS = [
+    (p, *block)
+    for p in range(len(PIECES))
+    for block in BLOCKS[1:]
+    if {"Z": block[0] == 0, "X": True, "J": block[0] != 0}[PIECES[p][0]]
+]
+KEY_ID = {key: n for n, key in enumerate(KEYS)}
 MOVED = NX * NZ - 1
-LATENCY, RATE, LEAD = 2.8, 46.6e3, 2.0
-STEP, ISSUE, MULTIPLY, SHARE = 0.03, 0.02, 0.47, 1.5
-READY = (0.0, 0.8, 0.8, 1.2, 0.8)
-X_FIRST_RANK = (0, 1, 2)
-X_RANK = (1, 2)
+LATENCY, Y_LATENCY, RATE, LEAD = 2.5, 3.0, 46.6e3, 1.85
+STEP, MULTIPLY, SHARE = 0.03, 0.47, 1.5
+READY = (0.0, 0.8, 1.2)
 BITS = (1.0, 12.0, 30.0)
-SUMS = (0.0, 4.2, 4.2)
+SUM = 3.8
+
+
+def rank_z(p, dx, dz):
+    return -1.0 if PIECES[p][0] == "Z" else abs(dx) - 0.6 * abs(dz)
+
+
+def rank_x(p, dx):
+    return {"X": (-1.0, 0.0), "J": (1.0, 2.0)}[PIECES[p][0]][abs(dx)]
 
 
 def program():
     free = dict.fromkeys(LINKS + ("y+", "y-"), 0.0)
     waiting = {link: [] for link in LINKS}
     inbox, ready, items, count = [], [], [], [0]
-    missing = {block: len(PIECES) for block in BLOCKS}
+    missing = {block: 2 if block[0] else len(PIECES) - 1 for block in BLOCKS}
+    unjoined = {dz: 2 for dx, dz in BLOCKS if dx == 0}
     left = {dx: NZ for dx in GROUP}
 
     def push(heap, when, what):
@@ -58,10 +69,10 @@
 
     def along_y(link, now, rows):
         free[link] = max(now, free[link]) + rows * 512 / RATE
-        return free[link] + LATENCY
+        return free[link] + Y_LATENCY
 
     def along_z(p, dx, dz):
-        rank = -1 if PIECES[p][0] else X_FIRST_RANK[abs(dx)]
+        rank = rank_z(p, dx, dz)
         if dz == 0:
             push(waiting["z+"], rank, (p, dx, -1))
             push(waiting["z-"], rank, (p, dx, 1))
@@ -74,12 +85,11 @@
                 push(waiting["z-" if dz > 0 else "z+"], rank, (p, dx, 4))
 
     def along_x(p, dx, dz):
+        rank = rank_x(p, dx) if abs(dx) < 2 else 0.0
         if dx == 0:
-            rank = X_RANK[0] if PIECES[p][0] else -1
             push(waiting["x+"], rank, (p, -1, dz))
             push(waiting["x-"], rank, (p, 1, dz))
         elif dx == (-1 if (p + dz) % 2 == 0 else 1):
-            rank = X_RANK[1] if PIECES[p][0] else 0
             push(waiting["x+" if dx < 0 else "x-"], rank, (p, 2, dz))
 
     for p, when in enumerate(READY):
@@ -88,14 +98,17 @@
         push(ready, when, ("bits", stage))
     push(ready, 3.0, ("weights", None))
     push(ready, 2.5, ("prepare", None))
-    now, stage = 0.0, 0
+    now = 0.0
     while inbox or ready:
         if inbox and inbox[0][0] <= now:
             key = heapq.heappop(inbox)[2]
             p, dx, dz = key
-            if PIECES[p][0]:
-                if dx == 0:
-                    along_z(*key)
+            if PIECES[p][0] == "Z":
+                along_z(*key)
+                unjoined[dz] -= 1
+                if unjoined[dz] == 0:
+                    along_x(JOINED, 0, dz)
+            elif PIECES[p][0] == "J":
                 along_x(*key)
             else:
                 if dz == 0:
@@ -103,7 +116,6 @@
                 along_z(*key)
             now += STEP
             sends = commit(now)
-            now += ISSUE * len(sends)
             items.append(("step", (key, sends)))
             block = dx, dz
             missing[block] -= 1
@@ -130,7 +142,7 @@
                 last = max(along_y("y+", now, 128), along_y("y-", now, 128))
                 push(ready, last, ("store", what))
             elif kind == "sum" and what < 2:
-                push(ready, now + SUMS[what + 1], ("sum", what + 1))
+                push(ready, now + SUM, ("sum", what + 1))
             elif kind == "prepare":
                 now += 0.3
             elif kind == "store":
@@ -140,7 +152,6 @@
                 items.append(("step", (None, sends)))
         else:
             now = min(heap[0][0] for heap in (inbox, ready) if heap)
-    program.end = now
     return items
 
 
@@ -270,7 +281,8 @@
         key, sends = what
         if key is not None:
             if key[1:] == (0, 0):
-                land(PIECES[key[0]][3])
+                for tile in PIECES[key[0]][3]:
+                    land(tile)
             else:
                 arrive(piece(key), piece_recv.at[KEY_ID[key]])
         for link, out in sends:
@@ -303,7 +315,8 @@
         fresh = group not in begun
         begun.add(group)
 
-        def pair(p, carry):
+        for p in range(2):
+
             def part(core, t):
                 return bg[at(xx, zz, core, (2 * p + t) * TILE, TILE), :]
 
@@ -314,9 +327,6 @@
             for t in range(2):
                 new_t = new[:, t * 128 : (t + 1) * 128]
                 acc[group, 2 * p + t] = new_t if fresh else acc[group, 2 * p + t] + new_t
-            return carry
-
-        lax.fori_loop(0, 2, pair, 0)
 
     def weights(_):
         for d in range(1, NY):
@@ -458,6 +468,19 @@
         move(0).wait_send()
 
 
+def hand_over(masked_ref, slot_ref, masked_out, slot_out, masked, slot, sem):
+    steps = ((masked_ref, masked, masked_out), (slot_ref, slot, slot_out))
+    ins = [pltpu.make_async_copy(a, b, sem.at[n]) for n, (a, b, _) in enumerate(steps)]
+    outs = [pltpu.make_async_copy(b, c, sem.at[2 + n]) for n, (_, b, c) in enumerate(steps)]
+    for copy in ins:
+        copy.start()
+    for came, copy in zip(ins, outs):
+        came.wait()
+        copy.start()
+    for copy in outs:
+        copy.wait()
+
+
 def on_device(a_values, a_present, b_values, b_present, w_values, w_present):
     hbm = pl.BlockSpec(memory_space=pltpu.HBM)
     smem = pl.BlockSpec(memory_space=pltpu.SMEM)
@@ -500,6 +523,19 @@
             collective_id=0, has_side_effects=True, vmem_limit_bytes=60 * 2**20
         ),
     )(a_values, a_present, b_values, b_present, w_values, w_present)
+    masked, slot = pl.pallas_call(
+        hand_over,
+        out_shape=(
+            jax.ShapeDtypeStruct((TILE, 512), bf16),
+            jax.ShapeDtypeStruct((1, 2), f32),
+        ),
+        in_specs=[hbm] * 2,
+        out_specs=(hbm, hbm),
+        scratch_shapes=[
+            pltpu.VMEM((TILE, 512), bf16), pltpu.VMEM((1, 2), f32), dma((4,)),
+        ],
+        compiler_params=pltpu.CompilerParams(vmem_limit_bytes=60 * 2**20),
+    )(masked, slot)
     return masked, slot, total.reshape(())
 
 

time: 83.7 us -> 79.9 us (0.955)
  local copies, waits for them, and re-layouts: 2.8 us -> 0 us
  Pallas kernels: 78.4 us -> 77.3 us
    pallas_call x1, Pallas kernels: 78.4 us -> 75.6 us  [on_device(): pl.pallas_call(kernel, out_shape=(jax.ShapeDtypeStruct((TILE, 512), bf16)...]
    unnamed x2 -> x0, local copies, waits for them, and re-layouts: 2.8 us -> none
    pallas_call x0 -> x1, Pallas kernels: none -> 1.69 us  [on_device(): pl.pallas_call(hand_over, out_shape=(jax.ShapeDtypeStruct((TILE, 512), bf...]
where the time goes in v4:
time: 79.9 us; the launch traced here: 79.7 us
  Pallas kernels  77.3 us (97%)
  between operations  2.46 us (3%)
    pallas_call x1, Pallas kernels, on_device(): pl.pallas_call(kernel, out_shape=(jax.ShapeDtypeStruct((TILE, 512), bf16)...  75.6 us
    pallas_call x1, Pallas kernels, on_device(): pl.pallas_call(hand_over, out_shape=(jax.ShapeDtypeStruct((TILE, 512), bf...  1.69 us

profile of v4, /device:TPU:1, one launch (start us, length us, event | category | flops | bytes accessed | tf_op | source)
XLA Modules:
  0.0 79.7 jit_solution(9568545178732655876)
XLA Ops:
  0.6 75.6 %shard_map.85 = (bf16[256,512]{1,0:T(8,128)(2,1)}, f32[1,2]{1,0:T(1,128)}, f32[1,1]{1,0:T(1,128)}) custom-call(bf16[256,4096]{1,0:T(8,128)(2,1)} %a_ref.1, s32[1,16]{1,0:T(1,128)} %ap_ref.1, bf16[256,512]{1,0:T(8,128)(2,1)} %b_ref.1, s32[1,2]{1,0:T(1,128)} %bp_ref.1, bf16[256,512]{1,0:T(8,128)(2,1)} %w_ref.1, s32[1,2]{1,0:T(1,128)} %wp_ref.1), custom_call_target="tpu_custom_call" | custom-call | tf_op jit(solution)/shard_map/pallas_call | solution.py:489
  76.2 1.7 %shard_map.86 = (bf16[256,512]{1,0:T(8,128)(2,1)}, f32[1,2]{1,0:T(1,128)}) custom-call(bf16[256,512]{1,0:T(8,128)(2,1)} %get-tuple-element.8.masked_ref, f32[1,2]{1,0:T(1,128)} %get-tuple-element.9.slot_ref), custom_call_target="tpu_custom_call" | custom-call | tf_op jit(solution)/shard_map/pallas_call | solution.py:526

commit v5 on v4

--- a/solution.py
+++ b/solution.py
@@ -158,8 +158,8 @@
 def kernel(
     a_ref, ap_ref, b_ref, bp_ref, w_ref, wp_ref,
     out_ref, slot_ref, total_ref,
-    bg, ae, acc, rl, rs, wa, bm, braw, wraw, masked, slots_v, tot, ixy, info, ta, ap, bp, wp,
-    a_sem, in_sem, out_sem, move_send, move_recv, bulk_send, piece_recv, share_recv,
+    bg, ae, acc, rl, rs, wa, bm, braw, wraw, tot, ixy, info, ta, ap, bp, wp,
+    a_sem, in_sem, move_send, move_recv, bulk_send, piece_recv, share_recv,
     w_send, w_recv, rs_send, rl_recv, rs_recv, info_send, info_recv, sum_send, sum_recv,
 ):
     row, y = lax.axis_index("row"), lax.axis_index("col")
@@ -365,21 +365,13 @@
             src, dst = acc.at[group, tile, half[part]], rs.at[group, side, half[part]]
             go(src, dst, rs_send, rs_recv.at[group], device(dy=d))
 
-    outs = []
-
-    def put(src, dst, n):
-        copy = pltpu.make_async_copy(src, dst, out_sem.at[n])
-        copy.start()
-        outs.append(copy)
-
     def store(dx):
         group, xx = GROUP[dx], block(dx, 0)[0]
         arrive(rs.at[group], rs_recv.at[group])
         value = acc[group, 0] + rs[group, 0] + rs[group, 1]
         value = value * wa[0, xx].astype(jnp.float32)
         cols = pl.ds(pl.multiple_of(xx * 128, 128), 128)
-        masked[group] = value.astype(jnp.bfloat16)
-        put(masked.at[group], out_ref.at[:, cols], group)
+        out_ref[:, cols] = value.astype(jnp.bfloat16)
 
     def bits_stage(stage):
         if stage == 0:
@@ -424,8 +416,7 @@
         slots = jnp.where(here > 0.5, before, -1.0)
         for t in range(2):
             here = jnp.where(lane == 64 + 2 * y + t, slots, 0.0)
-            slots_v[:, pl.ds(t, 1)] = jnp.sum(here, axis=1, keepdims=True)
-        put(slots_v, slot_ref, 4)
+            slot_ref[:, pl.ds(t, 1)] = jnp.sum(here, axis=1, keepdims=True)
 
     def sum_stage(k):
         if k == 0:
@@ -458,8 +449,6 @@
     gone(ixy.at[pl.ds(0, 15)], info_send.at[0])
     gone(info.at[pl.ds(0, 60)], info_send.at[1])
     gone(ta.at[pl.ds(0, 30)], sum_send)
-    for copy in outs:
-        copy.wait()
     for d in (1, 2, 3):
         move(d).wait_send()
 
@@ -468,22 +457,21 @@
         move(0).wait_send()
 
 
-def hand_over(masked_ref, slot_ref, masked_out, slot_out, masked, slot, sem):
-    steps = ((masked_ref, masked, masked_out), (slot_ref, slot, slot_out))
-    ins = [pltpu.make_async_copy(a, b, sem.at[n]) for n, (a, b, _) in enumerate(steps)]
-    outs = [pltpu.make_async_copy(b, c, sem.at[2 + n]) for n, (_, b, c) in enumerate(steps)]
-    for copy in ins:
+def hand_over(masked, slot, masked_out, slot_out, sem):
+    copies = [
+        pltpu.make_async_copy(src, dst, sem.at[n])
+        for n, (src, dst) in enumerate(((masked, masked_out), (slot, slot_out)))
+    ]
+    for copy in copies:
         copy.start()
-    for came, copy in zip(ins, outs):
-        came.wait()
-        copy.start()
-    for copy in outs:
+    for copy in copies:
         copy.wait()
 
 
 def on_device(a_values, a_present, b_values, b_present, w_values, w_present):
     hbm = pl.BlockSpec(memory_space=pltpu.HBM)
     smem = pl.BlockSpec(memory_space=pltpu.SMEM)
+    vmem = pl.BlockSpec(memory_space=pltpu.VMEM)
     dma = pltpu.SemaphoreType.DMA
     bf16, f32, i32 = jnp.bfloat16, jnp.float32, jnp.int32
     masked, slot, total = pl.pallas_call(
@@ -494,7 +482,7 @@
             jax.ShapeDtypeStruct((1, 1), f32),
         ),
         in_specs=[hbm] * 6,
-        out_specs=(hbm, hbm, smem),
+        out_specs=(vmem, vmem, smem),
         scratch_shapes=[
             pltpu.VMEM((NX * NZ * 2 * 1024, 128), bf16),
             pltpu.VMEM((NZ, TILE, 2 * TILE), bf16),
@@ -505,8 +493,6 @@
             pltpu.VMEM((NX, TILE, 128), bf16),
             pltpu.VMEM((TILE, 512), bf16),
             pltpu.VMEM((TILE, 512), bf16),
-            pltpu.VMEM((NX, TILE, 128), bf16),
-            pltpu.VMEM((1, 2), f32),
             pltpu.VMEM((8, 128), f32),
             pltpu.VMEM((NX * NY, 1, 128), f32),
             pltpu.VMEM((64, 1, 128), f32),
@@ -514,27 +500,28 @@
             pltpu.SMEM((1, 16), i32),
             pltpu.SMEM((1, 2), i32),
             pltpu.SMEM((1, 2), i32),
-            dma, dma((5,)), dma((5,)), dma((NX,)), dma((NY,)),
+            dma, dma((5,)), dma((NX,)), dma((NY,)),
             dma, dma((len(KEY_ID),)), dma((len(BLOCKS),)),
             dma, dma, dma, dma((NX,)), dma((NX,)),
             dma((2,)), dma((2,)), dma, dma((2,)),
         ],
         compiler_params=pltpu.CompilerParams(
-            collective_id=0, has_side_effects=True, vmem_limit_bytes=60 * 2**20
+            collective_id=0, has_side_effects=True, vmem_limit_bytes=48 * 2**20
         ),
-    )(a_values, a_present, b_values, b_present, w_values, w_present)
+    )(*[
+        pltpu.with_memory_space_constraint(v, pltpu.HBM)
+        for v in (a_values, a_present, b_values, b_present, w_values, w_present)
+    ])
     masked, slot = pl.pallas_call(
         hand_over,
         out_shape=(
             jax.ShapeDtypeStruct((TILE, 512), bf16),
             jax.ShapeDtypeStruct((1, 2), f32),
         ),
-        in_specs=[hbm] * 2,
+        in_specs=[vmem] * 2,
         out_specs=(hbm, hbm),
-        scratch_shapes=[
-            pltpu.VMEM((TILE, 512), bf16), pltpu.VMEM((1, 2), f32), dma((4,)),
-        ],
-        compiler_params=pltpu.CompilerParams(vmem_limit_bytes=60 * 2**20),
+        scratch_shapes=[dma((2,))],
+        compiler_params=pltpu.CompilerParams(vmem_limit_bytes=2**20),
     )(masked, slot)
     return masked, slot, total.reshape(())
 

time: 79.9 us -> 78.2 us (0.979)
  Pallas kernels: 77.3 us -> 75.6 us
    pallas_call x1, Pallas kernels: 1.69 us -> 0.72 us  [on_device(): pl.pallas_call(hand_over, out_shape=(jax.ShapeDtypeStruct((TILE, 512), bf...]
where the time goes in v5:
time: 78.2 us; the launch traced here: 78 us
  Pallas kernels  75.6 us (97%)
  between operations  2.41 us (3%)
    pallas_call x1, Pallas kernels, on_device(): pl.pallas_call(kernel, out_shape=(jax.ShapeDtypeStruct((TILE, 512), bf16)...  74.9 us

profile of v5, /device:TPU:1, one launch (start us, length us, event | category | flops | bytes accessed | tf_op | source)
XLA Modules:
  0.0 78.0 jit_solution(984920735110435630)
XLA Ops:
  0.6 74.9 %shard_map.85 = (bf16[256,512]{1,0:T(8,128)(2,1)S(1)}, f32[1,2]{1,0:T(1,128)S(1)}, f32[1,1]{1,0:T(1,128)}) custom-call(bf16[256,4096]{1,0:T(8,128)(2,1)} %a_ref.1, s32[1,16]{1,0:T(1,128)} %ap_ref.1, bf16[256,512]{1,0:T(8,128)(2,1)} %b_ref.1, s32[1,2]{1,0:T(1,128)} %bp_ref.1, bf16[256,512]{1,0:T(8,128)(2,1)} %w_ref.1, s32[1,2]{1,0:T(1,128)} %wp_ref.1), custom_call_target="tpu_custom_call" | custom-call | tf_op jit(solution)/shard_map/pallas_call | solution.py:477
  75.5 0.7 shard_map.86

commit v6 on v5

--- a/solution.py
+++ b/solution.py
@@ -120,7 +120,6 @@
             block = dx, dz
             missing[block] -= 1
             if missing[block] == 0:
-                items.append(("share", block))
                 push(ready, now + SHARE, ("multiply", block))
         elif ready and ready[0][0] <= now:
             kind, what = heapq.heappop(ready)[2]
@@ -290,11 +289,9 @@
             to = {"dx": d} if link[0] == "x" else {"dz": d}
             ref, n = piece(out, **to), KEY_ID[out]
             go(ref, ref, bulk_send, piece_recv.at[n], device(**to))
-
-    def share(what):
-        n, (xx, zz) = BLOCK_ID[what], block(*what)
-        ref = bg.at[at(xx, zz, c)]
-        go(ref, ref, bulk_send, share_recv.at[n], device(dc=1))
+        if key is not None:
+            ref, n = piece(key), BLOCK_ID[key[1:]]
+            go(ref, ref, bulk_send, share_recv.at[n], device(dc=1))
 
     def prepare(_):
         loads[4].wait()
@@ -437,7 +434,7 @@
             go(ref, ref, sum_send, sum_recv.at[k], device(**to))
 
     run = {
-        "step": step, "share": share, "prepare": prepare, "multiply": multiply,
+        "step": step, "prepare": prepare, "multiply": multiply,
         "weights": weights, "scatter": scatter, "add": add, "store": store,
         "bits": bits_stage, "sum": sum_stage,
     }

time: 78.2 us -> 78.1 us (level)
  no operation moved by 1% of the time
where the time goes in v6:
time: 78.1 us; the launch traced here: 78 us
  Pallas kernels  75.6 us (97%)
  between operations  2.41 us (3%)
    pallas_call x1, Pallas kernels, on_device(): pl.pallas_call(kernel, out_shape=(jax.ShapeDtypeStruct((TILE, 512), bf16)...  74.9 us

profile of v6, /device:TPU:1, one launch (start us, length us, event | category | flops | bytes accessed | tf_op | source)
XLA Modules:
  0.0 78.0 jit_solution(7498829589662383337)
XLA Ops:
  0.6 74.9 %shard_map.85 = (bf16[256,512]{1,0:T(8,128)(2,1)S(1)}, f32[1,2]{1,0:T(1,128)S(1)}, f32[1,1]{1,0:T(1,128)}) custom-call(bf16[256,4096]{1,0:T(8,128)(2,1)} %a_ref.1, s32[1,16]{1,0:T(1,128)} %ap_ref.1, bf16[256,512]{1,0:T(8,128)(2,1)} %b_ref.1, s32[1,2]{1,0:T(1,128)} %bp_ref.1, bf16[256,512]{1,0:T(8,128)(2,1)} %w_ref.1, s32[1,2]{1,0:T(1,128)} %wp_ref.1), custom_call_target="tpu_custom_call" | custom-call | tf_op jit(solution)/shard_map/pallas_call | solution.py:474
  75.5 0.7 shard_map.86
